TPU v7x, 256 devices: a whole 4x4x8 slice. The times are simulated.
256 devices in a mesh: wrow: 4 (over y), wcol: 16 (over z_hi, x), dom: 4 (over z_lo, core).
Axes of the slice: x: 4, y: 4, z: 8 (z_hi: 4, z_lo: 2; z = z_hi * 2 + z_lo), core: 2. Of those that a mesh axis runs over, the one named last changes fastest.
Arguments:
- positions: float32 [4, 16, 3, 8192], P('wrow', 'wcol', None, 'dom'), may hold values from -6 to 6
- velocities: float32 [4, 16, 3, 8192], P('wrow', 'wcol', None, 'dom'), may hold values from -6 to 6
- inv_mass: float32 [8192], P('dom'), may hold values from 0.5 to 2
- cv_weight: float32 [2, 3, 8192], P(None, None, 'dom'), may hold values from -0.125 to 0.125
- stiffness: float32 [2], replicated, may hold values from 1 to 4
- centers: float32 [4, 16, 2], P('wrow', 'wcol'), may hold values from -3 to 3
- block_order: int32 [8192], P('dom'), may hold values from 0 to 2047, as said below
- pair_count: int32 [4], P('dom'), may hold values from 16 to 64, as said below
- pair_own: int32 [4, 64], P('dom'), may hold values from 0 to 15, as said below
- pair_other: int32 [4, 64], P('dom'), may hold values from 0 to 47, as said below
- accept_row: int32 [4, 16], P('wrow', 'wcol'), may hold values from 0 to 1, as said below
- accept_col: int32 [4, 16], P('wrow', 'wcol'), may hold values from 0 to 1, as said below
Outputs:
- new_positions: float32 [4, 16, 3, 8192], P('wrow', 'wcol', None, 'dom')
- new_velocities: float32 [4, 16, 3, 8192], P('wrow', 'wcol', None, 'dom')
- new_forces: float32 [4, 16, 3, 8192], P('wrow', 'wcol', None, 'dom')
Inputs may be any that keep to these rules, and one draw needn't show every extreme that they name: accept_row is equal for windows (2k, c) and (2k + 1, c). accept_col is equal for windows (r, 2k) and (r, 2k + 1). `block_order`: each slab's 2048 entries are a permutation of 0 to 2047. `pair_count`: some slab has exactly 64 live pairs. `pair_own`: entries past the slab's pair_count are 0. `pair_other`: slab 0 names no lower slab and the last slab no upper slab; entries past the slab's pair_count are 16.
All inputs are finite; a program needn't handle non-finite values.
Results may differ from a plain program's by a relative error of at most 0.0003.
Values sent between devices are 32-bit elements; how exact they have to be, the bound alone decides.
A program may use at most 64 MiB of HBM per device.

v0:
```python
import math

import jax
import jax.numpy as jnp
from jax import lax
from jax.sharding import PartitionSpec as P

BLK = 128
STEPS = 3


PAIR_EPS = 0.015625
DT = 0.1


def copy_for_each(value, axis):
    length = lax.axis_size(axis)
    return lax.all_to_all(
        jnp.broadcast_to(value[None], (length, *value.shape)), axis, 0, 0, tiled=True
    )


def over_copies(value, axis):
    return copy_for_each(value, axis).sum(axis=0)


def extended(cells, sides, width):
    for axis, dim in sides:
        count = lax.axis_size(axis)
        ends = count - 1
        head = lax.slice_in_dim(cells, 0, width, axis=dim)
        tail = lax.slice_in_dim(cells, cells.shape[dim] - width, cells.shape[dim], axis=dim)
        cells = jnp.concatenate(
            [
                lax.ppermute(tail, axis, [(i, (i + 1) % count) for i in range(ends)]),
                cells,
                lax.ppermute(head, axis, [((i + 1) % count, i) for i in range(ends)]),
            ],
            axis=dim,
        )
    return cells


def from_partner(value, axis, apart):
    mask = 2**apart
    pairs = [(source, source ^ mask) for source in range(lax.axis_size(axis))]
    return lax.ppermute(value, axis, pairs)


def pair_batch(own_tiles, other_tiles):
    offsets = own_tiles[:, :, :, None] - other_tiles[:, :, None, :]
    squared = jnp.sum(offsets * offsets, axis=1)
    weight_tiles = PAIR_EPS * jnp.exp(-0.5 * squared)
    pulled = jnp.einsum("gcj,gij->gci", other_tiles, weight_tiles, precision=lax.Precision.HIGHEST)
    return own_tiles * jnp.sum(weight_tiles, axis=2)[:, None, :] - pulled


def per_device(
    positions,
    velocities,
    inv_mass,
    cv_weight,
    stiffness,
    centers,
    block_order,
    pair_count,
    pair_own,
    pair_other,
    accept_row,
    accept_col,
):
    atom_dev = block_order.shape[0]
    blocks_dev = atom_dev // BLK
    slots = pair_own.shape[1]
    group_size = math.gcd(slots, 32)
    groups = slots // group_size
    coords = positions[0, 0][:, block_order]
    speeds = velocities[0, 0][:, block_order]
    inverse_mass = inv_mass[block_order]
    weights = cv_weight[:, :, block_order]
    centre_pair = centers[0, 0]
    pair_total = pair_count[0]
    own_blocks = pair_own[0]
    other_blocks = pair_other[0]
    live_slots = jnp.arange(slots, dtype=jnp.int32) < pair_total
    owner_table = (
        (jnp.arange(blocks_dev, dtype=jnp.int32)[:, None] == own_blocks[None, :])
        & live_slots[None, :]
    ).astype(jnp.float32)

    def local_cv(current):
        return jnp.sum(weights * current[None], axis=(1, 2))

    def force_from(collective, nearby, centre_now):
        block_view = jnp.transpose(nearby.reshape(3, 3 * blocks_dev, BLK), (1, 0, 2))
        own_tiles = block_view[own_blocks + blocks_dev].reshape(groups, group_size, 3, BLK)
        other_tiles = block_view[other_blocks].reshape(groups, group_size, 3, BLK)
        tiles = lax.map(lambda pieces: pair_batch(pieces[0], pieces[1]), (own_tiles, other_tiles))
        tiles = tiles.reshape(slots, 3 * BLK)
        summed = jnp.dot(owner_table, tiles, precision=lax.Precision.HIGHEST)
        pair = jnp.transpose(summed.reshape(blocks_dev, 3, BLK), (1, 0, 2)).reshape(3, atom_dev)
        pull = stiffness * (collective - centre_now)
        return pair - jnp.sum(pull[:, None, None] * weights, axis=0)

    def total_force(current):
        collective = over_copies(local_cv(current), "dom")
        nearby = extended(current, (("dom", 1),), atom_dev)
        return force_from(collective, nearby, centre_pair)

    forces_now = total_force(coords)
    for _ in range(STEPS):
        speeds = speeds + 0.5 * DT * inverse_mass * forces_now
        coords = coords + DT * speeds
        forces_now = total_force(coords)
        speeds = speeds + 0.5 * DT * inverse_mass * forces_now
    inverse = (
        jnp.zeros((atom_dev,), jnp.int32).at[block_order].set(jnp.arange(atom_dev, dtype=jnp.int32))
    )
    stacked = jnp.stack([coords, speeds, forces_now])
    partner = from_partner(stacked, "wrow", 0)
    stacked = jnp.where(accept_row[0, 0] == 1, partner, stacked)
    partner = from_partner(stacked, "wcol", 0)
    stacked = jnp.where(accept_col[0, 0] == 1, partner, stacked)
    stacked = stacked[:, :, inverse]
    return (stacked[0][None, None], stacked[1][None, None], stacked[2][None, None])


def solution(mesh):
    placed = (
        P("wrow", "wcol", None, "dom"),
        P("wrow", "wcol", None, "dom"),
        P("dom"),
        P(None, None, "dom"),
        P(),
        P("wrow", "wcol", None),
        P("dom"),
        P("dom"),
        P("dom", None),
        P("dom", None),
        P("wrow", "wcol"),
        P("wrow", "wcol"),
    )
    return jax.shard_map(
        per_device,
        mesh=mesh,
        in_specs=placed,
        out_specs=(
            P("wrow", "wcol", None, "dom"),
            P("wrow", "wcol", None, "dom"),
            P("wrow", "wcol", None, "dom"),
        ),
        check_vma=False,
    )
```

profile of v0, /device:TPU:1, one launch (start us, length us, event | category | flops | bytes accessed | tf_op | source)
XLA Modules:
  0.0 240.5 jit_solution(14784190615666725362)
XLA Ops:
  3.1 5.5 %gather_fusion = f32[2048,3]{1,0:T(8,128)S(1)} fusion(f32[3,2048]{0,1:T(8,128)S(1)} %bitcast.293, s32[2048]{0:T(1024)S(1)} %get-tuple-element.169), kind=kCustom, calls=%fused_computation | custom fusion | bytes 57344 | tf_op jit(solution)/shard_map/gather | solution.py:77
  8.9 5.1 %collective-permute-start.1 = (f32[3,2048]{1,0:T(4,128)S(1)}, f32[3,2048]{1,0:T(4,128)S(1)}, u32[]{:S(2)}, u32[]{:S(2)}) collective-permute-start(f32[3,2048]{1,0:T(4,128)S(1)} %bitcast.294), channel_id=1, source_target_pairs={{1,0},{2,1},{3,2},{5,4},{6,5},{7,6},{9,8},{10,9},{11,10},{13,12},{... | collective-permute-start | bytes 73736 | tf_op jit(solution)/shard_map/ppermute | solution.py:37
  18.6 8.4 %gather_fusion.5 = f32[2048,2,3]{2,1,0:T(2,128)S(1)} fusion(f32[2,3,2048]{1,0,2:T(2,128)} %copy.260, s32[2048]{0:T(1024)S(1)} %get-tuple-element.169), kind=kCustom, calls=%fused_computation.5 | custom fusion | bytes 106496 | tf_op jit(solution)/shard_map/gather | solution.py:80
  30.0 3.9 %all-to-all-start = ((f32[4,1,2]{2,1,0:T(1,128)}), f32[4,1,2]{2,1,0:T(1,128)S(1)}, u32[]{:S(2)}, u32[]{:S(2)}) async-start(f32[4,1,2]{2,1,0:T(1,128)} %broadcast_in_dim.29), calls=%async_computation | async-start | bytes 4096 | tf_op jit(solution)/shard_map/all_to_all | solution.py:18
  34.6 11.8 %gather_fusion.2 = f32[2048]{0:T(1024)S(1)} fusion(f32[2048]{0:T(1024)S(1)} %copy-done, s32[2048]{0:T(1024)S(1)} %get-tuple-element.169), kind=kCustom, calls=%fused_computation.2 | custom fusion | bytes 24576 | tf_op jit(solution)/shard_map/gather | solution.py:79
  46.8 7.6 %gather_fusion.1 = f32[2048,3]{1,0:T(8,128)} fusion(f32[3,2048]{0,1:T(8,128)S(1)} %bitcast.292, s32[2048]{0:T(1024)S(1)} %get-tuple-element.169), kind=kCustom, calls=%fused_computation.1 | custom fusion | bytes 57344 | tf_op jit(solution)/shard_map/gather | solution.py:78
  56.0 9.9 %fusion.38 = f32[3,2048]{0,1:T(8,128)S(1)} fusion(f32[2048,2,3]{2,1,0:T(2,128)S(1)} %gather_fusion.5, f32[2]{0:T(128)S(1)} %fusion.71), kind=kLoop, calls=%fused_computation.76 | loop fusion | flops 18432 | bytes 73736 | tf_op jit(solution)/shard_map/reduce_sum | solution.py:103
  68.0 12.3 %while.40 = (s32[]{:T(128)}, f32[2,32,3,128]{3,2,1,0:T(4,128)S(1)}, f32[2,32,3,128]{3,2,1,0:T(4,128)S(1)}, f32[2,32,3,128]{3,2,1,0:T(4,128)S(1)}, s32[]{:T(128)}) while((s32[]{:T(128)}, f32[2,32,3,128]{3,2,1,0:T(4,128)S(1)}, f32[2,32,3,128]{3,2,1,0:T(4,128)S(1)}, f32[2,32,3,128]{3,2,1,0:T(4,128)S(1)}, s32[]{:T(128)}) %tuple.102), condition=%wide.region_3.0_spmd, body=%wide.region_0.3_spmd.sunk | while | flops 25710592 | bytes 6816841 | solution.py:98
  70.8 3.4 %fusion.89 = f32[2,32,3,128]{3,2,1,0:T(4,128)S(1)} fusion(f32[2,32,3,128]{3,2,1,0:T(4,128)S(1)} %get-tuple-element.292, s32[]{:T(128)S(6)} %copy.363, f32[32,128,128]{2,1,0:T(8,128)S(1)} %multiply_reduce_fusion.8, f32[32,128]{1,0:T(8,128)S(1)} %fusion.88, f32[2,32,3,128]{3,2,1,0:T(4,128)S(1)} %get-tuple-element.298, ...), kind=kOutput, calls=%fused_computation.20.clone.1 | convolution fusion | flops 19947520 | bytes 2311168 | tf_op jit(solution)/shard_map/while/body/eval_jaxpr/gcj,gij->gci/dot_general | solution.py:54
  76.9 3.4 %fusion.89 = f32[2,32,3,128]{3,2,1,0:T(4,128)S(1)} fusion(f32[2,32,3,128]{3,2,1,0:T(4,128)S(1)} %get-tuple-element.292, s32[]{:T(128)S(6)} %copy.363, f32[32,128,128]{2,1,0:T(8,128)S(1)} %multiply_reduce_fusion.8, f32[32,128]{1,0:T(8,128)S(1)} %fusion.88, f32[2,32,3,128]{3,2,1,0:T(4,128)S(1)} %get-tuple-element.298, ...), kind=kOutput, calls=%fused_computation.20.clone.1 | convolution fusion | flops 19947520 | bytes 2311168 | tf_op jit(solution)/shard_map/while/body/eval_jaxpr/gcj,gij->gci/dot_general | solution.py:54
  82.4 3.6 %collective-permute-start.2 = (f32[3,2048]{1,0:T(4,128)S(1)}, f32[3,2048]{1,0:T(4,128)S(1)}, u32[]{:S(2)}, u32[]{:S(2)}) collective-permute-start(f32[3,2048]{1,0:T(4,128)S(1)} %multiply_add_fusion.1), channel_id=1, source_target_pairs={{0,1},{1,2},{2,3},{4,5},{5,6},{6,7},{8,9},{9,10},{10,11},{12,13},{... | collective-permute-start | bytes 73736 | tf_op jit(solution)/shard_map/ppermute | solution.py:35
  88.7 5.2 %all_to_all.24 = f32[4,1,2]{2,1,0:T(1,128)S(1)} all-to-all(f32[4,1,2]{2,1,0:T(1,128)S(1)} %broadcast_in_dim.30), channel_id=1, replica_groups=mesh['wrow'=4,'wcol'=16,'dom'=4] {'dom'}, dimensions={0} | all-to-all | bytes 64 | tf_op jit(solution)/shard_map/all_to_all | solution.py:18
  94.0 9.9 %fusion.40 = f32[3,2048]{0,1:T(8,128)S(1)} fusion(f32[2048,2,3]{2,1,0:T(2,128)S(1)} %gather_fusion.5, f32[2]{0:T(128)S(1)} %fusion.72), kind=kLoop, calls=%fused_computation.78 | loop fusion | flops 18432 | bytes 73736 | tf_op jit(solution)/shard_map/reduce_sum | solution.py:103
  105.9 12.3 %while.41 = (s32[]{:T(128)}, f32[2,32,3,128]{3,2,1,0:T(4,128)S(1)}, f32[2,32,3,128]{3,2,1,0:T(4,128)S(1)}, f32[2,32,3,128]{3,2,1,0:T(4,128)S(1)}, s32[]{:T(128)}) while((s32[]{:T(128)}, f32[2,32,3,128]{3,2,1,0:T(4,128)S(1)}, f32[2,32,3,128]{3,2,1,0:T(4,128)S(1)}, f32[2,32,3,128]{3,2,1,0:T(4,128)S(1)}, s32[]{:T(128)}) %tuple.104), condition=%wide.region_10.11_spmd, body=%wide.region_7.0_spmd.sunk | while | flops 25710592 | bytes 6816841 | solution.py:98
  108.7 3.4 %fusion.91 = f32[2,32,3,128]{3,2,1,0:T(4,128)S(1)} fusion(f32[2,32,3,128]{3,2,1,0:T(4,128)S(1)} %get-tuple-element.307, s32[]{:T(128)S(6)} %copy.369, f32[32,128,128]{2,1,0:T(8,128)S(1)} %multiply_reduce_fusion.9, f32[32,128]{1,0:T(8,128)S(1)} %fusion.90, f32[2,32,3,128]{3,2,1,0:T(4,128)S(1)} %get-tuple-element.313, ...), kind=kOutput, calls=%fused_computation.33.clone.1 | convolution fusion | flops 19947520 | bytes 2311168 | tf_op jit(solution)/shard_map/while/body/eval_jaxpr/gcj,gij->gci/dot_general | solution.py:54
  114.8 3.4 %fusion.91 = f32[2,32,3,128]{3,2,1,0:T(4,128)S(1)} fusion(f32[2,32,3,128]{3,2,1,0:T(4,128)S(1)} %get-tuple-element.307, s32[]{:T(128)S(6)} %copy.369, f32[32,128,128]{2,1,0:T(8,128)S(1)} %multiply_reduce_fusion.9, f32[32,128]{1,0:T(8,128)S(1)} %fusion.90, f32[2,32,3,128]{3,2,1,0:T(4,128)S(1)} %get-tuple-element.313, ...), kind=kOutput, calls=%fused_computation.33.clone.1 | convolution fusion | flops 19947520 | bytes 2311168 | tf_op jit(solution)/shard_map/while/body/eval_jaxpr/gcj,gij->gci/dot_general | solution.py:54
  121.0 3.0 %collective-permute-start.4 = (f32[3,2048]{1,0:T(4,128)S(1)}, f32[3,2048]{1,0:T(4,128)S(1)}, u32[]{:S(2)}, u32[]{:S(2)}) collective-permute-start(f32[3,2048]{1,0:T(4,128)S(1)} %get-tuple-element.155), channel_id=1, source_target_pairs={{0,1},{1,2},{2,3},{4,5},{5,6},{6,7},{8,9},{9,10},{10,11},{12,13},{... | collective-permute-start | bytes 73736 | tf_op jit(solution)/shard_map/ppermute | solution.py:35
  126.7 5.3 %all_to_all.25 = f32[4,1,2]{2,1,0:T(1,128)S(1)} all-to-all(f32[4,1,2]{2,1,0:T(1,128)S(1)} %broadcast_in_dim.31), channel_id=1, replica_groups=mesh['wrow'=4,'wcol'=16,'dom'=4] {'dom'}, dimensions={0} | all-to-all | bytes 64 | tf_op jit(solution)/shard_map/all_to_all | solution.py:18
  132.1 9.9 %fusion.42 = f32[3,2048]{0,1:T(8,128)S(1)} fusion(f32[2048,2,3]{2,1,0:T(2,128)S(1)} %gather_fusion.5, f32[2]{0:T(128)S(1)} %fusion.73), kind=kLoop, calls=%fused_computation.80 | loop fusion | flops 18432 | bytes 73736 | tf_op jit(solution)/shard_map/reduce_sum | solution.py:103
  144.0 12.3 %while.42 = (s32[]{:T(128)}, f32[2,32,3,128]{3,2,1,0:T(4,128)S(1)}, f32[2,32,3,128]{3,2,1,0:T(4,128)S(1)}, f32[2,32,3,128]{3,2,1,0:T(4,128)S(1)}, s32[]{:T(128)}) while((s32[]{:T(128)}, f32[2,32,3,128]{3,2,1,0:T(4,128)S(1)}, f32[2,32,3,128]{3,2,1,0:T(4,128)S(1)}, f32[2,32,3,128]{3,2,1,0:T(4,128)S(1)}, s32[]{:T(128)}) %tuple.106), condition=%wide.region_17.18_spmd, body=%wide.region_14.0_spmd.sunk | while | flops 25710592 | bytes 6816841 | solution.py:98
  146.8 3.4 %fusion.93 = f32[2,32,3,128]{3,2,1,0:T(4,128)S(1)} fusion(f32[2,32,3,128]{3,2,1,0:T(4,128)S(1)} %get-tuple-element.322, s32[]{:T(128)S(6)} %copy.375, f32[32,128,128]{2,1,0:T(8,128)S(1)} %multiply_reduce_fusion.10, f32[32,128]{1,0:T(8,128)S(1)} %fusion.92, f32[2,32,3,128]{3,2,1,0:T(4,128)S(1)} %get-tuple-element.328, ...), kind=kOutput, calls=%fused_computation.46.clone.1 | convolution fusion | flops 19947520 | bytes 2311168 | tf_op jit(solution)/shard_map/while/body/eval_jaxpr/gcj,gij->gci/dot_general | solution.py:54
  152.9 3.4 %fusion.93 = f32[2,32,3,128]{3,2,1,0:T(4,128)S(1)} fusion(f32[2,32,3,128]{3,2,1,0:T(4,128)S(1)} %get-tuple-element.322, s32[]{:T(128)S(6)} %copy.375, f32[32,128,128]{2,1,0:T(8,128)S(1)} %multiply_reduce_fusion.10, f32[32,128]{1,0:T(8,128)S(1)} %fusion.92, f32[2,32,3,128]{3,2,1,0:T(4,128)S(1)} %get-tuple-element.328, ...), kind=kOutput, calls=%fused_computation.46.clone.1 | convolution fusion | flops 19947520 | bytes 2311168 | tf_op jit(solution)/shard_map/while/body/eval_jaxpr/gcj,gij->gci/dot_general | solution.py:54
  159.2 3.0 %collective-permute-start.6 = (f32[3,2048]{1,0:T(4,128)S(1)}, f32[3,2048]{1,0:T(4,128)S(1)}, u32[]{:S(2)}, u32[]{:S(2)}) collective-permute-start(f32[3,2048]{1,0:T(4,128)S(1)} %fusion.57), channel_id=1, source_target_pairs={{0,1},{1,2},{2,3},{4,5},{5,6},{6,7},{8,9},{9,10},{10,11},{12,13},{... | collective-permute-start | bytes 73736 | tf_op jit(solution)/shard_map/ppermute | solution.py:35
  165.4 3.4 %all-to-all-start.3 = ((f32[4,1,2]{2,1,0:T(1,128)}), f32[4,1,2]{2,1,0:T(1,128)S(1)}, u32[]{:S(2)}, u32[]{:S(2)}) async-start(f32[4,1,2]{2,1,0:T(1,128)} %broadcast_in_dim.32), calls=%async_computation.3 | async-start | bytes 4096 | tf_op jit(solution)/shard_map/all_to_all | solution.py:18
  171.3 9.9 %fusion.36 = f32[3,2048]{0,1:T(8,128)S(1)} fusion(f32[2048,2,3]{2,1,0:T(2,128)S(1)} %gather_fusion.5, f32[2]{0:T(128)S(1)} %fusion.74), kind=kLoop, calls=%fused_computation.74 | loop fusion | flops 18432 | bytes 73736 | tf_op jit(solution)/shard_map/reduce_sum | solution.py:103
  182.9 12.3 %while.43 = (s32[]{:T(128)}, f32[2,32,3,128]{3,2,1,0:T(4,128)S(1)}, f32[2,32,3,128]{3,2,1,0:T(4,128)S(1)}, f32[2,32,3,128]{3,2,1,0:T(4,128)S(1)}, s32[]{:T(128)}) while((s32[]{:T(128)}, f32[2,32,3,128]{3,2,1,0:T(4,128)S(1)}, f32[2,32,3,128]{3,2,1,0:T(4,128)S(1)}, f32[2,32,3,128]{3,2,1,0:T(4,128)S(1)}, s32[]{:T(128)}) %tuple.100), condition=%wide.region_24.25_spmd, body=%wide.region_21.0_spmd.sunk | while | flops 25710592 | bytes 6816841 | solution.py:98
  185.7 3.4 %fusion.95 = f32[2,32,3,128]{3,2,1,0:T(4,128)S(1)} fusion(f32[2,32,3,128]{3,2,1,0:T(4,128)S(1)} %get-tuple-element.337, s32[]{:T(128)S(6)} %copy.381, f32[32,128,128]{2,1,0:T(8,128)S(1)} %multiply_reduce_fusion.11, f32[32,128]{1,0:T(8,128)S(1)} %fusion.94, f32[2,32,3,128]{3,2,1,0:T(4,128)S(1)} %get-tuple-element.343, ...), kind=kOutput, calls=%fused_computation.59.clone.1 | convolution fusion | flops 19947520 | bytes 2311168 | tf_op jit(solution)/shard_map/while/body/eval_jaxpr/gcj,gij->gci/dot_general | solution.py:54
  191.8 3.4 %fusion.95 = f32[2,32,3,128]{3,2,1,0:T(4,128)S(1)} fusion(f32[2,32,3,128]{3,2,1,0:T(4,128)S(1)} %get-tuple-element.337, s32[]{:T(128)S(6)} %copy.381, f32[32,128,128]{2,1,0:T(8,128)S(1)} %multiply_reduce_fusion.11, f32[32,128]{1,0:T(8,128)S(1)} %fusion.94, f32[2,32,3,128]{3,2,1,0:T(4,128)S(1)} %get-tuple-element.343, ...), kind=kOutput, calls=%fused_computation.59.clone.1 | convolution fusion | flops 19947520 | bytes 2311168 | tf_op jit(solution)/shard_map/while/body/eval_jaxpr/gcj,gij->gci/dot_general | solution.py:54
  196.7 8.2 %scatter_custom_fusion = s32[2048]{0:T(1024)S(1)} fusion(s32[2048]{0:T(1024)} %get-tuple-element.168, s32[2048]{0:T(1024)S(1)} %iota.13, s32[]{:T(128)} %constant.73.clone.1), kind=kCustom, calls=%fused_computation.135 | custom fusion | bytes 8704 | tf_op jit(solution)/shard_map/scatter | solution.py:117
  209.0 3.1 %copy.288 = f32[3,3,2048]{1,0,2:T(4,128)} copy(f32[3,3,2048]{2,0,1:T(4,128)S(1)} %copy_select_fusion) | data formatting | bytes 147456 | tf_op jit(solution)/shard_map/jit(_where)/select_n | solution.py:123
  212.1 17.5 %gather_fusion.12 = f32[2048,3,3]{2,1,0:T(4,128)} fusion(f32[3,3,2048]{1,0,2:T(4,128)} %copy.288, s32[2048]{0:T(1024)S(1)} %fusion.64), kind=kCustom, calls=%fused_computation.12 | custom fusion | bytes 155648 | tf_op jit(solution)/shard_map/gather | solution.py:124
  229.7 7.8 %fusion.79 = (f32[1,3,2048]{1,0,2:T(1,128)S(1)}, f32[1,3,2048]{1,0,2:T(1,128)S(1)}, f32[1,3,2048]{1,0,2:T(1,128)S(1)}) fusion(f32[3,3,2048]{1,0,2:T(4,128)} %bitcast.291), kind=kLoop, calls=%fused_computation.150 | loop fusion | bytes 147456 | tf_op jit(solution)/shard_map/slice | solution.py:125
  (140 shorter events, 67.8 us)
Async XLA Ops:
  0.6 34.0 %copy-start = (f32[2048]{0:T(1024)S(1)}, f32[2048]{0:T(1024)}, u32[]{:S(2)}) copy-start(f32[2048]{0:T(1024)} %param.22) | copy-start | bytes 24580
  0.6 15.7 %copy-start.1 = (f32[2,3,2048]{2,0,1:T(2,128)S(1)}, f32[2,3,2048]{2,0,1:T(2,128)}, u32[]{:S(2)}) copy-start(f32[2,3,2048]{2,0,1:T(2,128)} %param.23) | copy-start | bytes 147460
  8.9 57.7 %collective-permute-start.1 = (f32[3,2048]{1,0:T(4,128)S(1)}, f32[3,2048]{1,0:T(4,128)S(1)}, u32[]{:S(2)}, u32[]{:S(2)}) collective-permute-start(f32[3,2048]{1,0:T(4,128)S(1)} %bitcast.294), channel_id=1, source_target_pairs={{1,0},{2,1},{3,2},{5,4},{6,5},{7,6},{9,8},{10,9},{11,10},{13,12},{... | collective-permute-start | bytes 73736 | tf_op jit(solution)/shard_map/ppermute | solution.py:37
  14.0 52.6 %collective-permute-start = (f32[3,2048]{1,0:T(4,128)S(1)}, f32[3,2048]{1,0:T(4,128)S(1)}, u32[]{:S(2)}, u32[]{:S(2)}) collective-permute-start(f32[3,2048]{1,0:T(4,128)S(1)} %bitcast.295), channel_id=1, source_target_pairs={{0,1},{1,2},{2,3},{4,5},{5,6},{6,7},{8,9},{9,10},{10,11},{12,13},{... | collective-permute-start | bytes 73736 | tf_op jit(solution)/shard_map/ppermute | solution.py:35
  18.6 15.9 %copy-start.11 = (s32[1,64]{1,0:T(1,128)S(1)}, s32[1,64]{1,0:T(1,128)}, u32[]{:S(2)}) copy-start(s32[1,64]{1,0:T(1,128)} %param.29) | copy-start | bytes 772
  18.6 15.9 %copy-start.3 = (s32[1,64]{1,0:T(1,128)S(1)}, s32[1,64]{1,0:T(1,128)}, u32[]{:S(2)}) copy-start(s32[1,64]{1,0:T(1,128)} %param.28) | copy-start | bytes 772
  30.0 26.0 %all-to-all-start = ((f32[4,1,2]{2,1,0:T(1,128)}), f32[4,1,2]{2,1,0:T(1,128)S(1)}, u32[]{:S(2)}, u32[]{:S(2)}) async-start(f32[4,1,2]{2,1,0:T(1,128)} %broadcast_in_dim.29), calls=%async_computation | async-start | bytes 4096 | tf_op jit(solution)/shard_map/all_to_all | solution.py:18
  34.5 83.7 %copy-start.5 = (pred[64]{0:T(512)(128)(4,1)}, pred[64]{0:T(512)(128)(4,1)S(1)}, u32[]{:S(2)}) copy-start(pred[64]{0:T(512)(128)(4,1)S(1)} %iota_compare_fusion.1) | copy-start | bytes 196
  34.6 11.8 %copy-start.2 = (f32[1,1,3,2048]{3,1,2,0:T(1,128)S(1)}, f32[1,1,3,2048]{3,1,2,0:T(1,128)}, u32[]{:S(2)}) copy-start(f32[1,1,3,2048]{3,1,2,0:T(1,128)} %param.21) | copy-start | bytes 73732
  46.4 9.6 %copy-start.7 = (f32[2]{0:T(128)S(1)}, f32[2]{0:T(128)}, u32[]{:S(2)}) copy-start(f32[2]{0:T(128)} %param.24) | copy-start | bytes 28
  46.4 9.6 %copy-start.9 = (f32[1,1,2]{2,1,0:T(1,128)S(1)}, f32[1,1,2]{2,1,0:T(1,128)}, u32[]{:S(2)}) copy-start(f32[1,1,2]{2,1,0:T(1,128)} %param.25) | copy-start | bytes 28
  80.5 24.0 %collective-permute-start.3 = (f32[3,2048]{1,0:T(4,128)S(1)}, f32[3,2048]{1,0:T(4,128)S(1)}, u32[]{:S(2)}, u32[]{:S(2)}) collective-permute-start(f32[3,2048]{1,0:T(4,128)S(1)} %multiply_add_fusion.1), channel_id=1, source_target_pairs={{1,0},{2,1},{3,2},{5,4},{6,5},{7,6},{9,8},{10,9},{11,10},{13,12},{... | collective-permute-start | bytes 73736 | tf_op jit(solution)/shard_map/ppermute | solution.py:37
  82.4 22.1 %collective-permute-start.2 = (f32[3,2048]{1,0:T(4,128)S(1)}, f32[3,2048]{1,0:T(4,128)S(1)}, u32[]{:S(2)}, u32[]{:S(2)}) collective-permute-start(f32[3,2048]{1,0:T(4,128)S(1)} %multiply_add_fusion.1), channel_id=1, source_target_pairs={{0,1},{1,2},{2,3},{4,5},{5,6},{6,7},{8,9},{9,10},{10,11},{12,13},{... | collective-permute-start | bytes 73736 | tf_op jit(solution)/shard_map/ppermute | solution.py:35
  118.4 24.2 %collective-permute-start.5 = (f32[3,2048]{1,0:T(4,128)S(1)}, f32[3,2048]{1,0:T(4,128)S(1)}, u32[]{:S(2)}, u32[]{:S(2)}) collective-permute-start(f32[3,2048]{1,0:T(4,128)S(1)} %get-tuple-element.155), channel_id=1, source_target_pairs={{1,0},{2,1},{3,2},{5,4},{6,5},{7,6},{9,8},{10,9},{11,10},{13,12},{... | collective-permute-start | bytes 73736 | tf_op jit(solution)/shard_map/ppermute | solution.py:37
  121.0 21.6 %collective-permute-start.4 = (f32[3,2048]{1,0:T(4,128)S(1)}, f32[3,2048]{1,0:T(4,128)S(1)}, u32[]{:S(2)}, u32[]{:S(2)}) collective-permute-start(f32[3,2048]{1,0:T(4,128)S(1)} %get-tuple-element.155), channel_id=1, source_target_pairs={{0,1},{1,2},{2,3},{4,5},{5,6},{6,7},{8,9},{9,10},{10,11},{12,13},{... | collective-permute-start | bytes 73736 | tf_op jit(solution)/shard_map/ppermute | solution.py:35
  144.0 12.3 %copy-start.4 = (s32[1,64]{1,0:T(1,128)S(1)}, s32[1,64]{1,0:T(1,128)}, u32[]{:S(2)}) copy-start(s32[1,64]{1,0:T(1,128)} %param.28) | copy-start | bytes 772
  144.0 12.3 %copy-start.6 = (pred[64]{0:T(512)(128)(4,1)S(1)}, pred[64]{0:T(512)(128)(4,1)}, u32[]{:S(2)}) copy-start(pred[64]{0:T(512)(128)(4,1)} %copy-done.5) | copy-start | bytes 196
  156.5 14.7 %copy-start.8 = (f32[2]{0:T(128)S(1)}, f32[2]{0:T(128)}, u32[]{:S(2)}) copy-start(f32[2]{0:T(128)} %param.24) | copy-start | bytes 28
  156.6 14.7 %copy-start.10 = (f32[1,1,2]{2,1,0:T(1,128)S(1)}, f32[1,1,2]{2,1,0:T(1,128)}, u32[]{:S(2)}) copy-start(f32[1,1,2]{2,1,0:T(1,128)} %param.25) | copy-start | bytes 28
  156.6 24.9 %collective-permute-start.7 = (f32[3,2048]{1,0:T(4,128)S(1)}, f32[3,2048]{1,0:T(4,128)S(1)}, u32[]{:S(2)}, u32[]{:S(2)}) collective-permute-start(f32[3,2048]{1,0:T(4,128)S(1)} %fusion.57), channel_id=1, source_target_pairs={{1,0},{2,1},{3,2},{5,4},{6,5},{7,6},{9,8},{10,9},{11,10},{13,12},{... | collective-permute-start | bytes 73736 | tf_op jit(solution)/shard_map/ppermute | solution.py:37
  159.2 22.3 %collective-permute-start.6 = (f32[3,2048]{1,0:T(4,128)S(1)}, f32[3,2048]{1,0:T(4,128)S(1)}, u32[]{:S(2)}, u32[]{:S(2)}) collective-permute-start(f32[3,2048]{1,0:T(4,128)S(1)} %fusion.57), channel_id=1, source_target_pairs={{0,1},{1,2},{2,3},{4,5},{5,6},{6,7},{8,9},{9,10},{10,11},{12,13},{... | collective-permute-start | bytes 73736 | tf_op jit(solution)/shard_map/ppermute | solution.py:35
  165.4 5.8 %all-to-all-start.3 = ((f32[4,1,2]{2,1,0:T(1,128)}), f32[4,1,2]{2,1,0:T(1,128)S(1)}, u32[]{:S(2)}, u32[]{:S(2)}) async-start(f32[4,1,2]{2,1,0:T(1,128)} %broadcast_in_dim.32), calls=%async_computation.3 | async-start | bytes 4096 | tf_op jit(solution)/shard_map/all_to_all | solution.py:18
  195.6 9.3 %collective-permute-start.8 = (f32[3,3,2048]{2,1,0:T(4,128)S(1)}, f32[3,3,2048]{2,1,0:T(4,128)S(1)}, u32[]{:S(2)}, u32[]{:S(2)}) collective-permute-start(f32[3,3,2048]{2,1,0:T(4,128)S(1)} %copy.284), channel_id=1, source_target_pairs={{0,64},{64,0},{128,192},{192,128},{1,65},{65,1},{129,193},{193,129... | collective-permute-start | bytes 221192 | tf_op jit(solution)/shard_map/ppermute | solution.py:47
  205.1 3.8 %collective-permute-start.9 = (f32[3,3,2048]{2,1,0:T(4,128)S(1)}, f32[3,3,2048]{2,1,0:T(4,128)S(1)}, u32[]{:S(2)}, u32[]{:S(2)}) collective-permute-start(f32[3,3,2048]{2,1,0:T(4,128)S(1)} %copy.286), channel_id=1, source_target_pairs={{0,4},{4,0},{8,12},{12,8},{16,20},{20,16},{24,28},{28,24},{32,36},... | collective-permute-start | bytes 221192 | tf_op jit(solution)/shard_map/ppermute | solution.py:47
where the time goes:
time: 245 us; the launch traced here: 241 us
  local copies, waits for them, and re-layouts  89.1 us (36%)
  other arithmetic  72.6 us (30%)
  starting transfers between devices  33 us (13%)
  matrix products  27.8 us (11%)
  blocking collectives  10.5 us (4%)
  waiting for transfers between devices  3.91 us (2%)
  between operations  3.44 us (1%)
    reduce_sum x4, other arithmetic, force_from(): return pair - jnp.sum(pull[:, None, None] * weights, axis=0)  39.5 us
    dot_general x8, matrix products, pair_batch(): jnp.einsum('gcj,gij->gci', other_tiles, weight_tiles, precision=lax.Preci...  27.1 us
    gather x1, local copies, waits for them, and re-layouts, per_device(): stacked = stacked[:, :, inverse]  17.5 us
    reduce_sum x8, other arithmetic, pair_batch(): squared = jnp.sum(offsets * offsets, axis=1)  16.6 us
    ppermute x4, starting transfers between devices, extended(): lax.ppermute(head, axis, [((i + 1) % count, i) for i in range(ends)])  12.3 us
    gather x1, local copies, waits for them, and re-layouts, per_device(): inverse_mass = inv_mass[block_order]  11.8 us
    ppermute x4, starting transfers between devices, extended(): lax.ppermute(tail, axis, [(i, (i + 1) % count) for i in range(ends)])  11.5 us
    all_to_all x2, blocking collectives, copy_for_each(): lax.all_to_all(jnp.broadcast_to(value[None], (length, *value.shape)), axi...  10.5 us
  transfers between devices with their start and end apart: 12, of which 2 were waited for; matrix products, arithmetic and copies ran while one was open for 39% of the time, Pallas kernels for 0%

commit v1 on v0

v1 whole, which is shorter than its diff:
```python
import functools
import math

import jax
import jax.numpy as jnp
from jax import lax
from jax.experimental import pallas as pl
from jax.experimental.pallas import tpu as pltpu
from jax.sharding import PartitionSpec as P

BLK = 128
STEPS = 3
EVALS = STEPS + 1
LOG2_EPS = -6.0
DT = 0.1
KAPPA = math.sqrt(0.5 * math.log2(math.e))
MESH = pl.DeviceIdType.MESH
VMEM = pltpu.VMEM
SMEM = pltpu.SMEM


def lane_take(rows, lanes):
    dims = lax.GatherDimensionNumbers(
        offset_dims=(),
        collapsed_slice_dims=(1,),
        start_index_map=(1,),
        operand_batching_dims=(0,),
        start_indices_batching_dims=(0,),
    )
    return lax.gather(
        rows, lanes[..., None], dims, slice_sizes=(1, 1), mode=lax.GatherScatterMode.PROMISE_IN_BOUNDS
    )


def permuted(source_row, blocks, index):
    halves = []
    for half in range(blocks // 8):
        piece = index[half * 8:(half + 1) * 8]
        lanes = piece & (BLK - 1)
        owner = piece >> 7
        total = jnp.zeros((8, BLK), jnp.float32)
        for s in range(blocks):
            taken = lane_take(jnp.broadcast_to(source_row(s), (8, BLK)), lanes)
            total = jnp.where(owner == s, taken, total)
        halves.append(total)
    return jnp.concatenate(halves, axis=0)


def split3(value):
    high = value.astype(jnp.bfloat16)
    rest = value - high.astype(jnp.float32)
    mid = rest.astype(jnp.bfloat16)
    low = (rest - mid.astype(jnp.float32)).astype(jnp.bfloat16)
    return high, mid, low


def pair_rows(near, own, other):
    other_row = near[pl.ds(other, 1), :]
    stacked = jnp.concatenate(
        [other_row[:, c * BLK:(c + 1) * BLK] for c in range(3)] + [jnp.zeros((5, BLK), jnp.float32)], axis=0
    )
    columns = stacked.T
    own_row = near[pl.ds(own, 1), :]
    mine = [jnp.broadcast_to(own_row[:, c * BLK:(c + 1) * BLK], (8, BLK)) for c in range(3)]
    sums = [jnp.zeros((8, BLK), jnp.float32) for _ in range(3)]
    for k in range(BLK // 8):
        rows = columns[k * 8:(k + 1) * 8]
        offsets = [mine[c] - jnp.broadcast_to(rows[:, c:c + 1], (8, BLK)) for c in range(3)]
        power = LOG2_EPS - offsets[0] * offsets[0]
        power = power - offsets[1] * offsets[1]
        power = power - offsets[2] * offsets[2]
        weight = jnp.exp2(power)
        sums = [sums[c] + weight * offsets[c] for c in range(3)]
    return [jnp.sum(sums[c], axis=0, keepdims=True) for c in range(3)]


def simulate(
    domains,
    slots,
    positions,
    velocities,
    inv_mass,
    cv_weight,
    block_order,
    own_lanes,
    stiffness,
    centers,
    pair_count,
    accept_row,
    accept_col,
    pair_own,
    pair_other,
    state_out,
    inverse_out,
    raw_x,
    raw_v,
    meta,
    chosen,
    x_ref,
    v_ref,
    f_ref,
    near_0,
    near_1,
    near_2,
    near_3,
    weights,
    mass,
    table,
    tiles,
    partial,
    in_sem,
    swap_send,
    swap_recv,
    halo_send,
    halo_recv,
    cv_send,
    cv_recv,
):
    row = lax.axis_index("wrow")
    col = lax.axis_index("wcol")
    dom = lax.axis_index("dom")
    blocks = block_order.shape[0]
    nears = (near_0, near_1, near_2, near_3)
    partners = [
        {"wrow": row ^ 1},
        {"wcol": col ^ 1},
        {"wrow": row ^ 1, "wcol": col ^ 1},
    ]
    peers = [{"dom": lax.rem(dom + k, domains)} for k in range(1, domains)]

    barrier = pltpu.get_barrier_semaphore()
    for device in partners + peers:
        pl.semaphore_signal(barrier, inc=1, device_id=device, device_id_type=MESH)
    own_x = pltpu.make_async_copy(positions, raw_x.at[0], in_sem.at[0])
    own_v = pltpu.make_async_copy(velocities, raw_v.at[0], in_sem.at[1])
    own_x.start()
    own_v.start()

    line = lax.broadcasted_iota(jnp.int32, (8, BLK), 0)
    meta[0] = jnp.where(
        line == 0, centers[0:1, 0:1], jnp.where(line == 1, centers[0:1, 1:2], accept_row[...].astype(jnp.float32))
    )

    own_x.wait()
    pl.semaphore_wait(barrier, len(partners) + len(peers))

    def swap(buffer, which):
        return [
            pltpu.make_async_remote_copy(
                src_ref=buffer.at[0],
                dst_ref=buffer.at[k + 1],
                send_sem=swap_send.at[which, k],
                recv_sem=swap_recv.at[which, k],
                device_id=partners[k],
                device_id_type=MESH,
            )
            for k in (2, 0, 1)
        ]

    moved_x, moved_v, moved_meta = swap(raw_x, 0), swap(raw_v, 1), swap(meta, 2)
    for copy in moved_meta:
        copy.start()
    for copy in moved_x:
        copy.start()
    own_v.wait()
    for copy in moved_v:
        copy.start()

    order = block_order[...]
    for k in range(2):
        for c in range(3):
            weights[k, :, c * BLK:(c + 1) * BLK] = permuted(
                lambda s: cv_weight[(c * blocks + s) * 2 + k:(c * blocks + s) * 2 + k + 1, :], blocks, order
            )
    mass_now = permuted(lambda s: inv_mass[s:s + 1, :], blocks, order)
    for c in range(3):
        mass[:, c * BLK:(c + 1) * BLK] = mass_now

    lane = lax.broadcasted_iota(jnp.int32, (blocks, BLK), 1)
    hi_line = lax.broadcasted_iota(jnp.int32, (blocks, BLK), 0)
    lo_line = lax.broadcasted_iota(jnp.int32, (BLK, BLK), 0)
    found = jnp.zeros((2 * blocks, BLK), jnp.float32)
    for b in range(blocks):
        atoms = order[b:b + 1]
        here = hi_line == (atoms >> 7)
        left = jnp.concatenate(
            [
                jnp.where(here, b, 0).astype(jnp.float32).astype(jnp.bfloat16),
                jnp.where(here, lane, 0).astype(jnp.float32).astype(jnp.bfloat16),
            ],
            axis=0,
        )
        right = jnp.where(lo_line == (atoms & (BLK - 1)), 1.0, 0.0).astype(jnp.bfloat16)
        found = found + lax.dot_general(left, right, (((1,), (1,)), ((), ())), preferred_element_type=jnp.float32)
    inverse_out[...] = (found[:blocks] * BLK + found[blocks:]).astype(jnp.int32)

    slot_lane = lax.broadcasted_iota(jnp.int32, (blocks, slots), 1)
    slot_line = lax.broadcasted_iota(jnp.int32, (blocks, slots), 0)
    listed = (own_lanes[...] == slot_line) & (slot_lane < pair_count[...])
    table[...] = jnp.where(listed, 1.0, 0.0).astype(jnp.bfloat16)

    for copy in moved_meta:
        copy.wait_recv()

    def choose(read):
        here = read(0)
        own_flag, col_flag = (jnp.broadcast_to(meta[k, 2:3, :], here.shape) for k in (0, 2))
        taken = jnp.broadcast_to(accept_col[...], here.shape)
        mine = jnp.where(own_flag == 1.0, read(1), here)
        theirs = jnp.where(col_flag == 1.0, read(3), read(2))
        return jnp.where(taken == 1, theirs, mine)

    def choose_all(buffer, target):
        chosen[...] = choose(lambda k: buffer[k])
        for c in range(3):
            target[:, c * BLK:(c + 1) * BLK] = permuted(
                lambda s: chosen[c * blocks + s:c * blocks + s + 1, :], blocks, order
            )

    centre = choose(lambda k: meta[k])

    for copy in moved_x:
        copy.wait_recv()
    choose_all(raw_x, x_ref)

    def halo(t):
        mine = nears[t].at[pl.ds(blocks, blocks), :]
        down = pltpu.make_async_remote_copy(
            src_ref=mine,
            dst_ref=nears[t].at[pl.ds(2 * blocks, blocks), :],
            send_sem=halo_send.at[t, 0],
            recv_sem=halo_recv.at[t, 0],
            device_id={"dom": lax.max(dom - 1, 0)},
            device_id_type=MESH,
        )
        up = pltpu.make_async_remote_copy(
            src_ref=mine,
            dst_ref=nears[t].at[pl.ds(0, blocks), :],
            send_sem=halo_send.at[t, 1],
            recv_sem=halo_recv.at[t, 1],
            device_id={"dom": lax.min(dom + 1, domains - 1)},
            device_id_type=MESH,
        )
        return down, up

    def shares(t):
        return [
            pltpu.make_async_remote_copy(
                src_ref=partial.at[t, 0],
                dst_ref=partial.at[t, k + 1],
                send_sem=cv_send.at[t, k],
                recv_sem=cv_recv.at[t, k],
                device_id=peers[k],
                device_id_type=MESH,
            )
            for k in range(domains - 1)
        ]

    has_lower = dom > 0
    has_upper = dom < domains - 1

    for t in range(EVALS):
        if t > 0:
            speeds = v_ref[...] + (0.5 * DT) * mass[...] * f_ref[...]
            v_ref[...] = speeds
            x_ref[...] = x_ref[...] + DT * speeds
        now = x_ref[...]
        nears[t][blocks:2 * blocks, :] = KAPPA * now
        down, up = halo(t)
        pl.when(has_lower)(down.start)
        pl.when(has_upper)(up.start)
        for k in range(2):
            product = weights[k] * now
            folded = product[:8] + product[8:]
            partial[t, 0, k * 8:(k + 1) * 8, :] = (
                folded[:, :BLK] + folded[:, BLK:2 * BLK] + folded[:, 2 * BLK:]
            )
        sent = shares(t)
        for copy in sent:
            copy.start()
        if t == 0:
            for copy in moved_v:
                copy.wait_recv()
            choose_all(raw_v, v_ref)
        pl.when(has_lower)(up.wait_recv)
        pl.when(has_upper)(down.wait_recv)

        def add_tile(p, carry):
            rows = pair_rows(nears[t], pair_own[0, p] + blocks, pair_other[0, p])
            for c in range(3):
                tiles[c, pl.ds(p, 1), :] = rows[c]
            return carry

        lax.fori_loop(0, slots, add_tile, 0, unroll=2)
        pair = jnp.zeros((blocks, 3 * BLK), jnp.float32)
        for piece in split3(jnp.concatenate([tiles[c] for c in range(3)], axis=1)):
            pair = pair + jnp.dot(table[...], piece, preferred_element_type=jnp.float32)
        force = (1.0 / KAPPA) * pair
        for copy in sent:
            copy.wait_recv()
        share = partial[t, 0]
        for k in range(1, domains):
            share = share + partial[t, k]
        for k in range(2):
            value = jnp.sum(
                jnp.sum(share[k * 8:(k + 1) * 8], axis=0, keepdims=True), axis=1, keepdims=True
            )
            force = force - (stiffness[0:1, k:k + 1] * (value - centre[k:k + 1, 0:1])) * weights[k]
        f_ref[...] = force
        if t > 0:
            v_ref[...] = v_ref[...] + (0.5 * DT) * mass[...] * force

    state_out[0:blocks, :] = x_ref[...]
    state_out[blocks:2 * blocks, :] = v_ref[...]
    state_out[2 * blocks:3 * blocks, :] = f_ref[...]

    for copy in moved_meta + moved_x + moved_v:
        copy.wait_send()
    for t in range(EVALS):
        down, up = halo(t)
        pl.when(has_lower)(down.wait_send)
        pl.when(has_upper)(up.wait_send)
        for copy in shares(t):
            copy.wait_send()


def restore(state, inverse, x_out, v_out, f_out):
    blocks = inverse.shape[0]
    index = inverse[...]
    for a, out in enumerate((x_out, v_out, f_out)):
        for c in range(3):
            value = permuted(
                lambda s: state[a * blocks + s:a * blocks + s + 1, c * BLK:(c + 1) * BLK], blocks, index
            )
            out[c * blocks:(c + 1) * blocks, :] = value


def per_device(
    domains,
    positions,
    velocities,
    inv_mass,
    cv_weight,
    stiffness,
    centers,
    block_order,
    pair_count,
    pair_own,
    pair_other,
    accept_row,
    accept_col,
):
    atoms = block_order.shape[0]
    blocks = atoms // BLK
    slots = pair_own.shape[1]
    f32 = jnp.float32
    vmem = pl.BlockSpec(memory_space=VMEM)
    smem = pl.BlockSpec(memory_space=SMEM)
    anywhere = pl.BlockSpec(memory_space=pl.ANY)
    dma = pltpu.SemaphoreType.DMA
    wide = 3 * BLK
    state, inverse = pl.pallas_call(
        functools.partial(simulate, domains, slots),
        out_shape=(
            jax.ShapeDtypeStruct((3 * blocks, wide), f32),
            jax.ShapeDtypeStruct((blocks, BLK), jnp.int32),
        ),
        in_specs=[anywhere] * 2 + [vmem] * 9 + [smem] * 2,
        out_specs=(vmem, vmem),
        scratch_shapes=[
            VMEM((4, 3 * blocks, BLK), f32),
            VMEM((4, 3 * blocks, BLK), f32),
            VMEM((4, 8, BLK), f32),
            VMEM((3 * blocks, BLK), f32),
            VMEM((blocks, wide), f32),
            VMEM((blocks, wide), f32),
            VMEM((blocks, wide), f32),
            VMEM((3 * blocks, wide), f32),
            VMEM((3 * blocks, wide), f32),
            VMEM((3 * blocks, wide), f32),
            VMEM((3 * blocks, wide), f32),
            VMEM((2, blocks, wide), f32),
            VMEM((blocks, wide), f32),
            VMEM((blocks, slots), jnp.bfloat16),
            VMEM((3, slots, BLK), f32),
            VMEM((EVALS, domains, 16, BLK), f32),
            dma((2,)),
            dma((3, 3)),
            dma((3, 3)),
            dma((EVALS, 2)),
            dma((EVALS, 2)),
            dma((EVALS, domains - 1)),
            dma((EVALS, domains - 1)),
        ],
        compiler_params=pltpu.CompilerParams(collective_id=0, has_side_effects=True),
        name="simulate",
    )(
        positions.reshape(3 * blocks, BLK),
        velocities.reshape(3 * blocks, BLK),
        inv_mass.reshape(blocks, BLK),
        cv_weight.reshape(2, 3, blocks, BLK).transpose(1, 2, 0, 3).reshape(6 * blocks, BLK),
        block_order.reshape(blocks, BLK),
        pair_own,
        stiffness[None],
        centers[0],
        pair_count[None],
        accept_row,
        accept_col,
        pair_own,
        pair_other,
    )
    outs = pl.pallas_call(
        restore,
        out_shape=(jax.ShapeDtypeStruct((3 * blocks, BLK), f32),) * 3,
        in_specs=[vmem] * 2,
        out_specs=(vmem,) * 3,
        name="restore",
    )(state, inverse)
    return tuple(out.reshape(1, 1, 3, atoms) for out in outs)


def solution(mesh):
    placed = (
        P("wrow", "wcol", None, "dom"),
        P("wrow", "wcol", None, "dom"),
        P("dom"),
        P(None, None, "dom"),
        P(),
        P("wrow", "wcol", None),
        P("dom"),
        P("dom"),
        P("dom", None),
        P("dom", None),
        P("wrow", "wcol"),
        P("wrow", "wcol"),
    )
    return jax.shard_map(
        functools.partial(per_device, mesh.shape["dom"]),
        mesh=mesh,
        in_specs=placed,
        out_specs=(P("wrow", "wcol", None, "dom"),) * 3,
        check_vma=False,
    )
```

time: 245 us -> 74.5 us (0.30); the launches traced: 241 us -> 74.2 us
  local copies, waits for them, and re-layouts: 89.1 us -> 0 us
  other arithmetic: 72.6 us -> 0 us
  Pallas kernels: 0 us -> 71.6 us
  starting transfers between devices: 33 us -> 0 us
  matrix products: 27.8 us -> 0 us
  blocking collectives: 10.5 us -> 0 us
  waiting for transfers between devices: 3.91 us -> 0 us
    pallas_call x0 -> x2, Pallas kernels: none -> 71.6 us  [the longest x1 69.7 us: per_device(): pl.pallas_call(functools.partial(simulate, domains, slots), out_shape=(ja...]
    reduce_sum x28 -> x0, other arithmetic: 70.4 us -> none  [the longest x4 39.5 us: force_from(): return pair - jnp.sum(pull[:, None, None] * weights, axis=0)]
    gather x16 -> x0, local copies, waits for them, and re-layouts: 58.3 us -> none  [the longest x1 17.5 us: per_device(): stacked = stacked[:, :, inverse]]
    dot_general x12 -> x0, matrix products: 27.8 us -> none  [the longest x8 27.1 us: pair_batch(): jnp.einsum('gcj,gij->gci', other_tiles, weight_tiles, precision=lax.Preci...]
    ppermute x10 -> x0, starting transfers between devices: 25.7 us -> none  [the longest x4 12.3 us: extended(): lax.ppermute(head, axis, [((i + 1) % count, i) for i in range(ends)])]
    all_to_all x2 -> x0, blocking collectives: 10.5 us -> none  [copy_for_each(): lax.all_to_all(jnp.broadcast_to(value[None], (length, *value.shape)), axi...]
    scatter x1 -> x0, local copies, waits for them, and re-layouts: 8.19 us -> none  [per_device(): jnp.zeros((atom_dev,), jnp.int32).at[block_order]]
    slice x1 -> x0, local copies, waits for them, and re-layouts: 7.83 us -> none  [per_device(): stacked[2][None, None]]
  transfers between devices with their start and end apart: 12 -> 0, of which waited for: 2 -> 0; matrix products, arithmetic and copies ran while one was open for 39% -> 0% of each run, Pallas kernels for 0% -> 0%
where the time goes in v1:
time: 74.5 us; the launch traced here: 74.2 us
  Pallas kernels  71.6 us (96%)
  between operations  2.58 us (3%)
    pallas_call x1, Pallas kernels, per_device(): pl.pallas_call(functools.partial(simulate, domains, slots), out_shape=(ja...  69.7 us
    pallas_call x1, Pallas kernels, per_device(): pl.pallas_call(restore, out_shape=(jax.ShapeDtypeStruct((3 * blocks, BLK)...  1.92 us

profile of v1, /device:TPU:1, one launch (start us, length us, event | category | flops | bytes accessed | tf_op | source)
XLA Modules:
  0.0 74.2 jit_solution(1591124923413470673)
XLA Ops:
  2.6 69.7 %simulate.1 = (f32[48,384]{1,0:T(8,128)}, s32[16,128]{1,0:T(8,128)}) custom-call(f32[48,128]{1,0:T(8,128)} %bitcast.17, f32[48,128]{1,0:T(8,128)} %bitcast.18, f32[16,128]{1,0:T(8,128)} %bitcast.19, f32[96,128]{1,0:T(8,128)} %bitcast.16, s32[16,128]{1,0:T(8,128)} %bitcast.20, s32[1,64]{1,0:T(1,128)} %pair_own.1, f32[1,2]{1,0:T(1,128)} %bitcast.21, ...), custom_call_target="tpu_custom_call" | custom-call | tf_op jit(solution)/shard_map/simulate/pallas_call | solution.py:362
  72.3 1.9 %restore.1 = (f32[48,128]{1,0:T(8,128)}, f32[48,128]{1,0:T(8,128)}, f32[48,128]{1,0:T(8,128)}) custom-call(f32[48,384]{1,0:T(8,128)} %get-tuple-element.8.state, s32[16,128]{1,0:T(8,128)} %get-tuple-element.9.inverse), custom_call_target="tpu_custom_call" | custom-call | tf_op jit(solution)/shard_map/restore/pallas_call | solution.py:412

commit v2 on v1

--- a/solution.py
+++ b/solution.py
@@ -11,9 +11,10 @@
 BLK = 128
 STEPS = 3
 EVALS = STEPS + 1
+UNROLL = 16
 LOG2_EPS = -6.0
 DT = 0.1
-KAPPA = math.sqrt(0.5 * math.log2(math.e))
+KAPPA = math.sqrt(math.log2(math.e))
 MESH = pl.DeviceIdType.MESH
 VMEM = pltpu.VMEM
 SMEM = pltpu.SMEM
@@ -54,24 +55,62 @@
     return high, mid, low
 
 
-def pair_rows(near, own, other):
-    other_row = near[pl.ds(other, 1), :]
-    stacked = jnp.concatenate(
-        [other_row[:, c * BLK:(c + 1) * BLK] for c in range(3)] + [jnp.zeros((5, BLK), jnp.float32)], axis=0
-    )
-    columns = stacked.T
-    own_row = near[pl.ds(own, 1), :]
-    mine = [jnp.broadcast_to(own_row[:, c * BLK:(c + 1) * BLK], (8, BLK)) for c in range(3)]
-    sums = [jnp.zeros((8, BLK), jnp.float32) for _ in range(3)]
-    for k in range(BLK // 8):
-        rows = columns[k * 8:(k + 1) * 8]
-        offsets = [mine[c] - jnp.broadcast_to(rows[:, c:c + 1], (8, BLK)) for c in range(3)]
-        power = LOG2_EPS - offsets[0] * offsets[0]
-        power = power - offsets[1] * offsets[1]
-        power = power - offsets[2] * offsets[2]
-        weight = jnp.exp2(power)
-        sums = [sums[c] + weight * offsets[c] for c in range(3)]
-    return [jnp.sum(sums[c], axis=0, keepdims=True) for c in range(3)]
+def split2(value):
+    high = value.astype(jnp.bfloat16)
+    return high, (value - high.astype(jnp.float32)).astype(jnp.bfloat16)
+
+
+def stack_groups(groups):
+    zero = jnp.zeros((8, BLK), jnp.float32)
+    upper = jnp.concatenate(groups[:2], axis=0).astype(jnp.bfloat16)
+    lower = jnp.concatenate([groups[2], zero], axis=0).astype(jnp.bfloat16)
+    return jnp.concatenate([upper, lower], axis=0)
+
+
+def parts(value):
+    return [piece.astype(jnp.float32) for piece in split3(value)]
+
+
+def partner_rows(rows, line):
+    high, mid, low = parts(rows)
+    middle = (line > 3) & (line < 7)
+    return stack_groups(
+        [
+            high,
+            jnp.where(line < 4, mid, jnp.where(line == 7, high, low)),
+            jnp.where(line == 3, low, jnp.where(middle, mid, high)),
+        ]
+    )
+
+
+def owner_rows(rows, line):
+    high, mid, low = parts(rows)
+    middle = (line > 3) & (line < 7)
+    return stack_groups(
+        [
+            jnp.where(middle, mid, high),
+            jnp.where(line == 7, mid, high),
+            jnp.where(line == 3, high, jnp.where(middle, mid, low)),
+        ]
+    )
+
+
+def two_tiles(partners, owners, other, own):
+    left = [partners[q] for q in other]
+    right = [owners[b] for b in own]
+    zero = jnp.zeros_like(right[0])
+    power = lax.dot_general(
+        jnp.concatenate(left, axis=0),
+        jnp.concatenate(
+            [jnp.concatenate([right[0], zero], axis=1), jnp.concatenate([zero, right[1]], axis=1)], axis=0
+        ),
+        (((0,), (0,)), ((), ())),
+        preferred_element_type=jnp.float32,
+    )
+    weight = jnp.concatenate(split2(jnp.exp2(jnp.minimum(power, LOG2_EPS))), axis=0)
+    heads = [jnp.concatenate([rows[:16], rows[:16]], axis=1) for rows in left]
+    sums = jnp.dot(jnp.concatenate(heads, axis=0), weight, preferred_element_type=jnp.float32)
+    return sums[:16, :BLK], sums[16:, BLK:]
 
 
 def simulate(
@@ -107,6 +146,8 @@
     mass,
     table,
     tiles,
+    partners_tab,
+    owners_tab,
     partial,
     in_sem,
     swap_send,
@@ -120,6 +161,7 @@
     col = lax.axis_index("wcol")
     dom = lax.axis_index("dom")
     blocks = block_order.shape[0]
+    rows_slab = 4 * blocks
     nears = (near_0, near_1, near_2, near_3)
     partners = [
         {"wrow": row ^ 1},
@@ -224,10 +266,10 @@
     choose_all(raw_x, x_ref)
 
     def halo(t):
-        mine = nears[t].at[pl.ds(blocks, blocks), :]
+        mine = nears[t].at[pl.ds(rows_slab, rows_slab), :]
         down = pltpu.make_async_remote_copy(
             src_ref=mine,
-            dst_ref=nears[t].at[pl.ds(2 * blocks, blocks), :],
+            dst_ref=nears[t].at[pl.ds(2 * rows_slab, rows_slab), :],
             send_sem=halo_send.at[t, 0],
             recv_sem=halo_recv.at[t, 0],
             device_id={"dom": lax.max(dom - 1, 0)},
@@ -235,7 +277,7 @@
         )
         up = pltpu.make_async_remote_copy(
             src_ref=mine,
-            dst_ref=nears[t].at[pl.ds(0, blocks), :],
+            dst_ref=nears[t].at[pl.ds(0, rows_slab), :],
             send_sem=halo_send.at[t, 1],
             recv_sem=halo_recv.at[t, 1],
             device_id={"dom": lax.min(dom + 1, domains - 1)},
@@ -265,7 +307,10 @@
             v_ref[...] = speeds
             x_ref[...] = x_ref[...] + DT * speeds
         now = x_ref[...]
-        nears[t][blocks:2 * blocks, :] = KAPPA * now
+        scaled = [KAPPA * now[:, c * BLK:(c + 1) * BLK] for c in range(3)]
+        norm = -0.5 * (scaled[0] * scaled[0] + scaled[1] * scaled[1] + scaled[2] * scaled[2])
+        for c, rows in enumerate(scaled + [norm]):
+            nears[t][pl.ds(rows_slab + c, blocks, stride=4), :] = rows
         down, up = halo(t)
         pl.when(has_lower)(down.start)
         pl.when(has_upper)(up.start)
@@ -282,20 +327,48 @@
             for copy in moved_v:
                 copy.wait_recv()
             choose_all(raw_v, v_ref)
+
+        def block_rows(b):
+            four = nears[t][4 * b:4 * b + 4, :]
+            return jnp.concatenate([four, four], axis=0)
+
+        for b in range(blocks):
+            rows = block_rows(blocks + b)
+            partners_tab[blocks + b] = partner_rows(jnp.where(line == 7, 1.0, rows), line)
+            owners_tab[b] = owner_rows(
+                jnp.where(line == 3, 1.0, jnp.where(line == 7, rows + LOG2_EPS, rows)), line
+            )
         pl.when(has_lower)(up.wait_recv)
         pl.when(has_upper)(down.wait_recv)
-
-        def add_tile(p, carry):
-            rows = pair_rows(nears[t], pair_own[0, p] + blocks, pair_other[0, p])
-            for c in range(3):
-                tiles[c, pl.ds(p, 1), :] = rows[c]
+        for b in list(range(blocks)) + list(range(2 * blocks, 3 * blocks)):
+            partners_tab[b] = partner_rows(jnp.where(line == 7, 1.0, block_rows(b)), line)
+
+        def add_tiles(group, carry):
+            for u in range(UNROLL):
+                first = group * (2 * UNROLL) + 2 * u
+                sums = two_tiles(
+                    partners_tab,
+                    owners_tab,
+                    [pair_other[0, first + k] for k in range(2)],
+                    [pair_own[0, first + k] for k in range(2)],
+                )
+                for k in range(2):
+                    tiles[pl.ds(pl.multiple_of(16 * (first + k), 16), 16), :] = sums[k]
             return carry
 
-        lax.fori_loop(0, slots, add_tile, 0, unroll=2)
-        pair = jnp.zeros((blocks, 3 * BLK), jnp.float32)
-        for piece in split3(jnp.concatenate([tiles[c] for c in range(3)], axis=1)):
+        lax.fori_loop(0, slots // (2 * UNROLL), add_tiles, 0)
+
+        def slot_rows(r):
+            return tiles[pl.ds(r, slots, stride=16), :]
+
+        listed_rows = jnp.concatenate(
+            [slot_rows(c) + slot_rows(8 + c) + slot_rows(12 + c) for c in range(3)] + [slot_rows(7)], axis=1
+        )
+        pair = jnp.zeros((blocks, 4 * BLK), jnp.float32)
+        for piece in split3(listed_rows):
             pair = pair + jnp.dot(table[...], piece, preferred_element_type=jnp.float32)
-        force = (1.0 / KAPPA) * pair
+        total = pair[:, 3 * BLK:]
+        force = now * jnp.concatenate([total, total, total], axis=1) - (1.0 / KAPPA) * pair[:, :3 * BLK]
         for copy in sent:
             copy.wait_recv()
         share = partial[t, 0]
@@ -375,14 +448,16 @@
             VMEM((blocks, wide), f32),
             VMEM((blocks, wide), f32),
             VMEM((blocks, wide), f32),
-            VMEM((3 * blocks, wide), f32),
-            VMEM((3 * blocks, wide), f32),
-            VMEM((3 * blocks, wide), f32),
-            VMEM((3 * blocks, wide), f32),
+            VMEM((12 * blocks, BLK), f32),
+            VMEM((12 * blocks, BLK), f32),
+            VMEM((12 * blocks, BLK), f32),
+            VMEM((12 * blocks, BLK), f32),
             VMEM((2, blocks, wide), f32),
             VMEM((blocks, wide), f32),
             VMEM((blocks, slots), jnp.bfloat16),
-            VMEM((3, slots, BLK), f32),
+            VMEM((16 * slots, BLK), f32),
+            VMEM((3 * blocks, 32, BLK), jnp.bfloat16),
+            VMEM((blocks, 32, BLK), jnp.bfloat16),
             VMEM((EVALS, domains, 16, BLK), f32),
             dma((2,)),
             dma((3, 3)),

time: 74.5 us -> 32.9 us (0.44)
  Pallas kernels: 71.6 us -> 30.1 us
    pallas_call x1, Pallas kernels: 69.7 us -> 28.2 us  [per_device(): pl.pallas_call(functools.partial(simulate, domains, slots), out_shape=(ja...]
where the time goes in v2:
time: 32.9 us; the launch traced here: 32.7 us
  Pallas kernels  30.1 us (91%)
  between operations  2.58 us (8%)
    pallas_call x1, Pallas kernels, per_device(): pl.pallas_call(functools.partial(simulate, domains, slots), out_shape=(ja...  28.2 us
    pallas_call x1, Pallas kernels, per_device(): pl.pallas_call(restore, out_shape=(jax.ShapeDtypeStruct((3 * blocks, BLK)...  1.92 us

profile of v2, /device:TPU:1, one launch (start us, length us, event | category | flops | bytes accessed | tf_op | source)
XLA Modules:
  0.0 32.7 jit_solution(15280320063322693473)
XLA Ops:
  2.6 28.2 %simulate.1 = (f32[48,384]{1,0:T(8,128)}, s32[16,128]{1,0:T(8,128)}) custom-call(f32[48,128]{1,0:T(8,128)} %bitcast.17, f32[48,128]{1,0:T(8,128)} %bitcast.18, f32[16,128]{1,0:T(8,128)} %bitcast.19, f32[96,128]{1,0:T(8,128)} %bitcast.16, s32[16,128]{1,0:T(8,128)} %bitcast.20, s32[1,64]{1,0:T(1,128)} %pair_own.1, f32[1,2]{1,0:T(1,128)} %bitcast.21, ...), custom_call_target="tpu_custom_call" | custom-call | tf_op jit(solution)/shard_map/simulate/pallas_call | solution.py:435
  30.7 1.9 %restore.1 = (f32[48,128]{1,0:T(8,128)}, f32[48,128]{1,0:T(8,128)}, f32[48,128]{1,0:T(8,128)}) custom-call(f32[48,384]{1,0:T(8,128)} %get-tuple-element.8.state, s32[16,128]{1,0:T(8,128)} %get-tuple-element.9.inverse), custom_call_target="tpu_custom_call" | custom-call | tf_op jit(solution)/shard_map/restore/pallas_call | solution.py:487

commit v3 on v2

--- a/solution.py
+++ b/solution.py
@@ -11,7 +11,7 @@
 BLK = 128
 STEPS = 3
 EVALS = STEPS + 1
-UNROLL = 16
+UNROLL = 32
 LOG2_EPS = -6.0
 DT = 0.1
 KAPPA = math.sqrt(math.log2(math.e))
@@ -113,56 +113,20 @@
     return sums[:16, :BLK], sums[16:, BLK:]
 
 
-def simulate(
-    domains,
-    slots,
-    positions,
-    velocities,
-    inv_mass,
-    cv_weight,
-    block_order,
-    own_lanes,
-    stiffness,
-    centers,
-    pair_count,
-    accept_row,
-    accept_col,
-    pair_own,
-    pair_other,
-    state_out,
-    inverse_out,
-    raw_x,
-    raw_v,
-    meta,
-    chosen,
-    x_ref,
-    v_ref,
-    f_ref,
-    near_0,
-    near_1,
-    near_2,
-    near_3,
-    weights,
-    mass,
-    table,
-    tiles,
-    partners_tab,
-    owners_tab,
-    partial,
-    in_sem,
-    swap_send,
-    swap_recv,
-    halo_send,
-    halo_recv,
-    cv_send,
-    cv_recv,
-):
+def simulate(domains, slots, *refs):
+    inputs, refs = refs[:13], refs[13:]
+    (state_out, inverse_out), refs = refs[:2], refs[2:]
+    local, refs = refs[:11], refs[11:]
+    inv_mass, cv_weight, block_order, own_lanes, stiffness, centers, pair_count = local[:7]
+    accept_row, accept_col, pair_own, pair_other = local[7:]
+    raw_x, raw_v, meta, chosen, x_ref, v_ref, f_ref, near = refs[:8]
+    weights, mass, table, tiles, partners_tab, owners_tab, partial = refs[8:15]
+    in_sem, swap_send, swap_recv, halo_send, halo_recv, cv_send, cv_recv = refs[15:]
     row = lax.axis_index("wrow")
     col = lax.axis_index("wcol")
     dom = lax.axis_index("dom")
     blocks = block_order.shape[0]
     rows_slab = 4 * blocks
-    nears = (near_0, near_1, near_2, near_3)
     partners = [
         {"wrow": row ^ 1},
         {"wcol": col ^ 1},
@@ -173,10 +137,15 @@
     barrier = pltpu.get_barrier_semaphore()
     for device in partners + peers:
         pl.semaphore_signal(barrier, inc=1, device_id=device, device_id_type=MESH)
-    own_x = pltpu.make_async_copy(positions, raw_x.at[0], in_sem.at[0])
-    own_v = pltpu.make_async_copy(velocities, raw_v.at[0], in_sem.at[1])
-    own_x.start()
-    own_v.start()
+    arrivals = [
+        pltpu.make_async_copy(source, target, in_sem.at[k])
+        for k, (source, target) in enumerate(zip(inputs, (raw_x.at[0], raw_v.at[0]) + local))
+    ]
+    for k in (0, 7, 9, 1, 4, 2, 3, 5, 6, 8, 10, 11, 12):
+        arrivals[k].start()
+    own_x, own_v = arrivals[:2]
+    arrivals[7].wait()
+    arrivals[9].wait()
 
     line = lax.broadcasted_iota(jnp.int32, (8, BLK), 0)
     meta[0] = jnp.where(
@@ -208,6 +177,8 @@
     for copy in moved_v:
         copy.start()
 
+    for k in (4, 2, 3, 5, 6, 8, 10, 11, 12):
+        arrivals[k].wait()
     order = block_order[...]
     for k in range(2):
         for c in range(3):
@@ -266,10 +237,10 @@
     choose_all(raw_x, x_ref)
 
     def halo(t):
-        mine = nears[t].at[pl.ds(rows_slab, rows_slab), :]
+        mine = near.at[t, pl.ds(rows_slab, rows_slab), :]
         down = pltpu.make_async_remote_copy(
             src_ref=mine,
-            dst_ref=nears[t].at[pl.ds(2 * rows_slab, rows_slab), :],
+            dst_ref=near.at[t, pl.ds(2 * rows_slab, rows_slab), :],
             send_sem=halo_send.at[t, 0],
             recv_sem=halo_recv.at[t, 0],
             device_id={"dom": lax.max(dom - 1, 0)},
@@ -277,7 +248,7 @@
         )
         up = pltpu.make_async_remote_copy(
             src_ref=mine,
-            dst_ref=nears[t].at[pl.ds(0, rows_slab), :],
+            dst_ref=near.at[t, pl.ds(0, rows_slab), :],
             send_sem=halo_send.at[t, 1],
             recv_sem=halo_recv.at[t, 1],
             device_id={"dom": lax.min(dom + 1, domains - 1)},
@@ -301,8 +272,9 @@
     has_lower = dom > 0
     has_upper = dom < domains - 1
 
-    for t in range(EVALS):
-        if t > 0:
+    def evaluate(t, carry):
+        @pl.when(t > 0)
+        def _():
             speeds = v_ref[...] + (0.5 * DT) * mass[...] * f_ref[...]
             v_ref[...] = speeds
             x_ref[...] = x_ref[...] + DT * speeds
@@ -310,26 +282,26 @@
         scaled = [KAPPA * now[:, c * BLK:(c + 1) * BLK] for c in range(3)]
         norm = -0.5 * (scaled[0] * scaled[0] + scaled[1] * scaled[1] + scaled[2] * scaled[2])
         for c, rows in enumerate(scaled + [norm]):
-            nears[t][pl.ds(rows_slab + c, blocks, stride=4), :] = rows
+            near[t, pl.ds(rows_slab + c, blocks, stride=4), :] = rows
         down, up = halo(t)
         pl.when(has_lower)(down.start)
         pl.when(has_upper)(up.start)
         for k in range(2):
             product = weights[k] * now
             folded = product[:8] + product[8:]
-            partial[t, 0, k * 8:(k + 1) * 8, :] = (
-                folded[:, :BLK] + folded[:, BLK:2 * BLK] + folded[:, 2 * BLK:]
-            )
+            folded = folded[:, :BLK] + folded[:, BLK:2 * BLK] + folded[:, 2 * BLK:]
+            partial[t, 0, k:k + 1, :] = jnp.sum(folded, axis=0, keepdims=True)
         sent = shares(t)
         for copy in sent:
             copy.start()
-        if t == 0:
+        @pl.when(t == 0)
+        def _():
             for copy in moved_v:
                 copy.wait_recv()
             choose_all(raw_v, v_ref)
 
         def block_rows(b):
-            four = nears[t][4 * b:4 * b + 4, :]
+            four = near[t, 4 * b:4 * b + 4, :]
             return jnp.concatenate([four, four], axis=0)
 
         for b in range(blocks):
@@ -375,13 +347,16 @@
         for k in range(1, domains):
             share = share + partial[t, k]
         for k in range(2):
-            value = jnp.sum(
-                jnp.sum(share[k * 8:(k + 1) * 8], axis=0, keepdims=True), axis=1, keepdims=True
-            )
+            value = jnp.sum(share[k:k + 1], axis=1, keepdims=True)
             force = force - (stiffness[0:1, k:k + 1] * (value - centre[k:k + 1, 0:1])) * weights[k]
         f_ref[...] = force
-        if t > 0:
+        @pl.when(t > 0)
+        def _():
             v_ref[...] = v_ref[...] + (0.5 * DT) * mass[...] * force
+
+        return carry
+
+    lax.fori_loop(0, EVALS, evaluate, 0)
 
     state_out[0:blocks, :] = x_ref[...]
     state_out[blocks:2 * blocks, :] = v_ref[...]
@@ -428,8 +403,7 @@
     slots = pair_own.shape[1]
     f32 = jnp.float32
     vmem = pl.BlockSpec(memory_space=VMEM)
-    smem = pl.BlockSpec(memory_space=SMEM)
-    anywhere = pl.BlockSpec(memory_space=pl.ANY)
+    anywhere = pl.BlockSpec(memory_space=pltpu.HBM)
     dma = pltpu.SemaphoreType.DMA
     wide = 3 * BLK
     state, inverse = pl.pallas_call(
@@ -438,9 +412,20 @@
             jax.ShapeDtypeStruct((3 * blocks, wide), f32),
             jax.ShapeDtypeStruct((blocks, BLK), jnp.int32),
         ),
-        in_specs=[anywhere] * 2 + [vmem] * 9 + [smem] * 2,
+        in_specs=[anywhere] * 13,
         out_specs=(vmem, vmem),
         scratch_shapes=[
+            VMEM((blocks, BLK), f32),
+            VMEM((6 * blocks, BLK), f32),
+            VMEM((blocks, BLK), jnp.int32),
+            VMEM((1, slots), jnp.int32),
+            VMEM((1, 2), f32),
+            VMEM((1, 2), f32),
+            VMEM((1, 1), jnp.int32),
+            VMEM((1, 1), jnp.int32),
+            VMEM((1, 1), jnp.int32),
+            SMEM((1, slots), jnp.int32),
+            SMEM((1, slots), jnp.int32),
             VMEM((4, 3 * blocks, BLK), f32),
             VMEM((4, 3 * blocks, BLK), f32),
             VMEM((4, 8, BLK), f32),
@@ -448,18 +433,15 @@
             VMEM((blocks, wide), f32),
             VMEM((blocks, wide), f32),
             VMEM((blocks, wide), f32),
-            VMEM((12 * blocks, BLK), f32),
-            VMEM((12 * blocks, BLK), f32),
-            VMEM((12 * blocks, BLK), f32),
-            VMEM((12 * blocks, BLK), f32),
+            VMEM((EVALS, 12 * blocks, BLK), f32),
             VMEM((2, blocks, wide), f32),
             VMEM((blocks, wide), f32),
             VMEM((blocks, slots), jnp.bfloat16),
             VMEM((16 * slots, BLK), f32),
             VMEM((3 * blocks, 32, BLK), jnp.bfloat16),
             VMEM((blocks, 32, BLK), jnp.bfloat16),
-            VMEM((EVALS, domains, 16, BLK), f32),
-            dma((2,)),
+            VMEM((EVALS, domains, 2, BLK), f32),
+            dma((13,)),
             dma((3, 3)),
             dma((3, 3)),
             dma((EVALS, 2)),

time: 32.9 us -> 30.6 us (0.930)
  Pallas kernels: 30.1 us -> 27.9 us
    pallas_call x1, Pallas kernels: 28.2 us -> 25.9 us  [per_device(): pl.pallas_call(functools.partial(simulate, domains, slots), out_shape=(ja...]
where the time goes in v3:
time: 30.6 us; the launch traced here: 30.4 us
  Pallas kernels  27.9 us (91%)
  between operations  2.58 us (8%)
    pallas_call x1, Pallas kernels, per_device(): pl.pallas_call(functools.partial(simulate, domains, slots), out_shape=(ja...  25.9 us
    pallas_call x1, Pallas kernels, per_device(): pl.pallas_call(restore, out_shape=(jax.ShapeDtypeStruct((3 * blocks, BLK)...  1.92 us

profile of v3, /device:TPU:1, one launch (start us, length us, event | category | flops | bytes accessed | tf_op | source)
XLA Modules:
  0.0 30.4 jit_solution(1894046130994142402)
XLA Ops:
  2.6 25.9 %simulate.1 = (f32[48,384]{1,0:T(8,128)}, s32[16,128]{1,0:T(8,128)}) custom-call(f32[48,128]{1,0:T(8,128)} %bitcast.17, f32[48,128]{1,0:T(8,128)} %bitcast.18, f32[16,128]{1,0:T(8,128)} %bitcast.19, f32[96,128]{1,0:T(8,128)} %bitcast.16, s32[16,128]{1,0:T(8,128)} %bitcast.20, s32[1,64]{1,0:T(1,128)} %refs_11_.1, f32[1,2]{1,0:T(1,128)} %bitcast.21, ...), custom_call_target="tpu_custom_call" | custom-call | tf_op jit(solution)/shard_map/simulate/pallas_call | solution.py:409
  28.5 1.9 %restore.1 = (f32[48,128]{1,0:T(8,128)}, f32[48,128]{1,0:T(8,128)}, f32[48,128]{1,0:T(8,128)}) custom-call(f32[48,384]{1,0:T(8,128)} %get-tuple-element.8.state, s32[16,128]{1,0:T(8,128)} %get-tuple-element.9.inverse), custom_call_target="tpu_custom_call" | custom-call | tf_op jit(solution)/shard_map/restore/pallas_call | solution.py:469

commit v4 on v3

--- a/solution.py
+++ b/solution.py
@@ -381,6 +381,10 @@
                 lambda s: state[a * blocks + s:a * blocks + s + 1, c * BLK:(c + 1) * BLK], blocks, index
             )
             out[c * blocks:(c + 1) * blocks, :] = value
+
+
+def hbm(x):
+    return x if x.size == 1 else pltpu.with_memory_space_constraint(x, pltpu.HBM)
 
 
 def per_device(
@@ -449,9 +453,10 @@
             dma((EVALS, domains - 1)),
             dma((EVALS, domains - 1)),
         ],
-        compiler_params=pltpu.CompilerParams(collective_id=0, has_side_effects=True),
+        compiler_params=pltpu.CompilerParams(collective_id=0, has_side_effects=True, vmem_limit_bytes=16 * 2**20),
         name="simulate",
     )(
+        *map(hbm, (
         positions.reshape(3 * blocks, BLK),
         velocities.reshape(3 * blocks, BLK),
         inv_mass.reshape(blocks, BLK),
@@ -465,12 +470,14 @@
         accept_col,
         pair_own,
         pair_other,
+        ))
     )
     outs = pl.pallas_call(
         restore,
         out_shape=(jax.ShapeDtypeStruct((3 * blocks, BLK), f32),) * 3,
         in_specs=[vmem] * 2,
         out_specs=(vmem,) * 3,
+        compiler_params=pltpu.CompilerParams(vmem_limit_bytes=8 * 2**20),
         name="restore",
     )(state, inverse)
     return tuple(out.reshape(1, 1, 3, atoms) for out in outs)

time: 30.6 us -> 29.1 us (0.951)
  Pallas kernels: 27.9 us -> 26.3 us
    pallas_call x1, Pallas kernels: 1.92 us -> 1.04 us  [per_device(): pl.pallas_call(restore, out_shape=(jax.ShapeDtypeStruct((3 * blocks, BLK)...]
    pallas_call x1, Pallas kernels: 25.9 us -> 25.3 us  [per_device(): pl.pallas_call(functools.partial(simulate, domains, slots), out_shape=(ja...]
where the time goes in v4:
time: 29.1 us; the launch traced here: 28.9 us
  Pallas kernels  26.3 us (90%)
  between operations  2.58 us (9%)
    pallas_call x1, Pallas kernels, per_device(): pl.pallas_call(functools.partial(simulate, domains, slots), out_shape=(ja...  25.3 us
    pallas_call x1, Pallas kernels, per_device(): pl.pallas_call(restore, out_shape=(jax.ShapeDtypeStruct((3 * blocks, BLK)...  1.04 us

profile of v4, /device:TPU:1, one launch (start us, length us, event | category | flops | bytes accessed | tf_op | source)
XLA Modules:
  0.0 28.9 jit_solution(10715249681209840364)
XLA Ops:
  2.6 25.3 %simulate.1 = (f32[48,384]{1,0:T(8,128)S(1)}, s32[16,128]{1,0:T(8,128)S(1)}) custom-call(f32[48,128]{1,0:T(8,128)} %bitcast.17, f32[48,128]{1,0:T(8,128)} %bitcast.18, f32[16,128]{1,0:T(8,128)} %bitcast.19, f32[96,128]{1,0:T(8,128)} %bitcast.16, s32[16,128]{1,0:T(8,128)} %bitcast.20, s32[1,64]{1,0:T(1,128)} %refs_11_.1, f32[1,2]{1,0:T(1,128)} %bitcast.21, ...), custom_call_target="tpu_custom_call" | custom-call | tf_op jit(solution)/shard_map/simulate/pallas_call | solution.py:413
  27.9 1.0 %restore.1 = (f32[48,128]{1,0:T(8,128)}, f32[48,128]{1,0:T(8,128)}, f32[48,128]{1,0:T(8,128)}) custom-call(f32[48,384]{1,0:T(8,128)S(1)} %get-tuple-element.8.state, s32[16,128]{1,0:T(8,128)S(1)} %get-tuple-element.9.inverse), custom_call_target="tpu_custom_call" | custom-call | tf_op jit(solution)/shard_map/restore/pallas_call | solution.py:475

commit v5 on v4

--- a/solution.py
+++ b/solution.py
@@ -114,23 +114,33 @@
 
 
 def simulate(domains, slots, *refs):
-    inputs, refs = refs[:13], refs[13:]
+    inputs, refs = refs[:12], refs[12:]
     (state_out, inverse_out), refs = refs[:2], refs[2:]
     local, refs = refs[:11], refs[11:]
-    inv_mass, cv_weight, block_order, own_lanes, stiffness, centers, pair_count = local[:7]
-    accept_row, accept_col, pair_own, pair_other = local[7:]
-    raw_x, raw_v, meta, chosen, x_ref, v_ref, f_ref, near = refs[:8]
-    weights, mass, table, tiles, partners_tab, owners_tab, partial = refs[8:15]
-    in_sem, swap_send, swap_recv, halo_send, halo_recv, cv_send, cv_recv = refs[15:]
+    inv_mass, cv_weight, block_order, own_lanes, other_lanes, stiffness, centers = local[:7]
+    pair_count, accept_row, accept_col, named = local[7:]
+    home_x, home_v, raw_x, raw_v, meta, fresh, x_ref, v_ref, f_ref, near = refs[:10]
+    weights, mass, lists, table, tiles, partners_tab, owners_tab, partial = refs[10:18]
+    in_sem, list_sem, swap_send, swap_recv, twin_send, twin_recv = refs[18:24]
+    halo_send, halo_recv, cv_send, cv_recv = refs[24:]
     row = lax.axis_index("wrow")
     col = lax.axis_index("wcol")
     dom = lax.axis_index("dom")
     blocks = block_order.shape[0]
     rows_slab = 4 * blocks
+    last = EVALS - 1
+
+    def place(d):
+        return d ^ (d >> 1)
+
+    spot = place(dom)
+    moved = spot != dom
+    role = jnp.where(moved, 1, 0)
+    twin = {"dom": spot}
     partners = [
-        {"wrow": row ^ 1},
-        {"wcol": col ^ 1},
-        {"wrow": row ^ 1, "wcol": col ^ 1},
+        {"wrow": row ^ 1, "dom": spot},
+        {"wcol": col ^ 1, "dom": spot},
+        {"wrow": row ^ 1, "wcol": col ^ 1, "dom": spot},
     ]
     peers = [{"dom": lax.rem(dom + k, domains)} for k in range(1, domains)]
 
@@ -139,26 +149,41 @@
         pl.semaphore_signal(barrier, inc=1, device_id=device, device_id_type=MESH)
     arrivals = [
         pltpu.make_async_copy(source, target, in_sem.at[k])
-        for k, (source, target) in enumerate(zip(inputs, (raw_x.at[0], raw_v.at[0]) + local))
+        for k, (source, target) in enumerate(zip(inputs, (fresh.at[0], fresh.at[1]) + local[:10]))
     ]
-    for k in (0, 7, 9, 1, 4, 2, 3, 5, 6, 8, 10, 11, 12):
+    for k in (4, 0, 8, 10, 1, 2, 3, 5, 6, 7, 9, 11):
         arrivals[k].start()
     own_x, own_v = arrivals[:2]
-    arrivals[7].wait()
-    arrivals[9].wait()
+    arrivals[8].wait()
+    arrivals[10].wait()
 
     line = lax.broadcasted_iota(jnp.int32, (8, BLK), 0)
     meta[0] = jnp.where(
         line == 0, centers[0:1, 0:1], jnp.where(line == 1, centers[0:1, 1:2], accept_row[...].astype(jnp.float32))
     )
 
+    arrivals[4].wait()
+    order = block_order[...]
+
+    def reorder(which, target):
+        for c in range(3):
+            target[c * blocks:(c + 1) * blocks, :] = permuted(
+                lambda s: fresh[which, c * blocks + s:c * blocks + s + 1, :], blocks, order
+            )
+
     own_x.wait()
+    reorder(0, home_x)
+
+    @pl.when(jnp.logical_not(moved))
+    def _():
+        raw_x[0] = home_x[...]
+
     pl.semaphore_wait(barrier, len(partners) + len(peers))
 
-    def swap(buffer, which):
+    def swap(source, buffer, which):
         return [
             pltpu.make_async_remote_copy(
-                src_ref=buffer.at[0],
+                src_ref=source,
                 dst_ref=buffer.at[k + 1],
                 send_sem=swap_send.at[which, k],
                 recv_sem=swap_recv.at[which, k],
@@ -168,26 +193,60 @@
             for k in (2, 0, 1)
         ]
 
-    moved_x, moved_v, moved_meta = swap(raw_x, 0), swap(raw_v, 1), swap(meta, 2)
+    def to_twin(source, target, k):
+        return pltpu.make_async_remote_copy(
+            src_ref=source,
+            dst_ref=target,
+            send_sem=twin_send.at[k],
+            recv_sem=twin_recv.at[k],
+            device_id=twin,
+            device_id_type=MESH,
+        )
+
+    moved_x, moved_v = swap(home_x, raw_x, 0), swap(home_v, raw_v, 1)
+    moved_meta = swap(meta.at[0], meta, 2)
+    twin_x, twin_v = to_twin(home_x, raw_x.at[0], 0), to_twin(home_v, raw_v.at[0], 1)
+    twin_rest = [
+        to_twin(weights.at[0], weights.at[1], 2),
+        to_twin(mass.at[0], mass.at[1], 3),
+        to_twin(lists.at[0], lists.at[1], 4),
+    ]
+    twin_state = [to_twin(x_ref.at[1], x_ref.at[0], 5), to_twin(v_ref.at[1], v_ref.at[0], 6)]
     for copy in moved_meta:
         copy.start()
     for copy in moved_x:
         copy.start()
+    pl.when(moved)(twin_x.start)
     own_v.wait()
+    reorder(1, home_v)
+
+    @pl.when(jnp.logical_not(moved))
+    def _():
+        raw_v[0] = home_v[...]
+
     for copy in moved_v:
         copy.start()
-
-    for k in (4, 2, 3, 5, 6, 8, 10, 11, 12):
+    pl.when(moved)(twin_v.start)
+
+    for k in (2, 3, 5, 6, 7, 9, 11):
         arrivals[k].wait()
-    order = block_order[...]
     for k in range(2):
         for c in range(3):
-            weights[k, :, c * BLK:(c + 1) * BLK] = permuted(
+            weights[0, k, :, c * BLK:(c + 1) * BLK] = permuted(
                 lambda s: cv_weight[(c * blocks + s) * 2 + k:(c * blocks + s) * 2 + k + 1, :], blocks, order
             )
     mass_now = permuted(lambda s: inv_mass[s:s + 1, :], blocks, order)
     for c in range(3):
-        mass[:, c * BLK:(c + 1) * BLK] = mass_now
+        mass[0, :, c * BLK:(c + 1) * BLK] = mass_now
+    gap = jnp.zeros((1, BLK - slots), jnp.int32)
+    listing = [jnp.concatenate([rows[...], gap], axis=1) for rows in (own_lanes, other_lanes)]
+    lists[0] = jnp.where(line == 0, listing[0], jnp.where(line == 1, listing[1], pair_count[...]))
+
+    @pl.when(moved)
+    def _():
+        for copy in twin_rest:
+            copy.start()
+
 
     lane = lax.broadcasted_iota(jnp.int32, (blocks, BLK), 1)
     hi_line = lax.broadcasted_iota(jnp.int32, (blocks, BLK), 0)
@@ -207,10 +266,16 @@
         found = found + lax.dot_general(left, right, (((1,), (1,)), ((), ())), preferred_element_type=jnp.float32)
     inverse_out[...] = (found[:blocks] * BLK + found[blocks:]).astype(jnp.int32)
 
-    slot_lane = lax.broadcasted_iota(jnp.int32, (blocks, slots), 1)
-    slot_line = lax.broadcasted_iota(jnp.int32, (blocks, slots), 0)
-    listed = (own_lanes[...] == slot_line) & (slot_lane < pair_count[...])
-    table[...] = jnp.where(listed, 1.0, 0.0).astype(jnp.bfloat16)
+    def use_lists(which):
+        slot_lane = lax.broadcasted_iota(jnp.int32, (blocks, slots), 1)
+        slot_line = lax.broadcasted_iota(jnp.int32, (blocks, slots), 0)
+        listed = (lists[which, 0:1, :slots] == slot_line) & (slot_lane < lists[which, 2:3, :slots])
+        table[which] = jnp.where(listed, 1.0, 0.0).astype(jnp.bfloat16)
+        copy = pltpu.make_async_copy(lists.at[which], named.at[which], list_sem.at[which])
+        copy.start()
+        copy.wait()
+
+    use_lists(0)
 
     for copy in moved_meta:
         copy.wait_recv()
@@ -224,37 +289,49 @@
         return jnp.where(taken == 1, theirs, mine)
 
     def choose_all(buffer, target):
-        chosen[...] = choose(lambda k: buffer[k])
+        picked = choose(lambda k: buffer[k])
         for c in range(3):
-            target[:, c * BLK:(c + 1) * BLK] = permuted(
-                lambda s: chosen[c * blocks + s:c * blocks + s + 1, :], blocks, order
-            )
+            target[role, :, c * BLK:(c + 1) * BLK] = picked[c * blocks:(c + 1) * blocks]
 
     centre = choose(lambda k: meta[k])
 
     for copy in moved_x:
         copy.wait_recv()
+    pl.when(moved)(twin_x.wait_recv)
     choose_all(raw_x, x_ref)
 
+    @pl.when(moved)
+    def _():
+        for copy in twin_rest:
+            copy.wait_recv()
+        use_lists(1)
+
+
+    def frame(t):
+        return jnp.where(t == last, dom, spot)
+
+    def mine_at(t):
+        return pl.multiple_of((spot - frame(t) + 1) * rows_slab, rows_slab)
+
     def halo(t):
-        mine = near.at[t, pl.ds(rows_slab, rows_slab), :]
-        down = pltpu.make_async_remote_copy(
-            src_ref=mine,
-            dst_ref=near.at[t, pl.ds(2 * rows_slab, rows_slab), :],
-            send_sem=halo_send.at[t, 0],
-            recv_sem=halo_recv.at[t, 0],
-            device_id={"dom": lax.max(dom - 1, 0)},
-            device_id_type=MESH,
-        )
-        up = pltpu.make_async_remote_copy(
-            src_ref=mine,
-            dst_ref=near.at[t, pl.ds(0, rows_slab), :],
-            send_sem=halo_send.at[t, 1],
-            recv_sem=halo_recv.at[t, 1],
-            device_id={"dom": lax.min(dom + 1, domains - 1)},
-            device_id_type=MESH,
-        )
-        return down, up
+        sides = []
+        for side in range(3):
+            target = spot - (side - 1)
+            device = jnp.where(t == last, target, place(jnp.clip(target, 0, domains - 1)))
+            device = jnp.clip(device, 0, domains - 1)
+            inside = (target >= 0) & (target < domains)
+            copy = pltpu.make_async_remote_copy(
+                src_ref=near.at[t, pl.ds(mine_at(t), rows_slab), :],
+                dst_ref=near.at[t, pl.ds(side * rows_slab, rows_slab), :],
+                send_sem=halo_send.at[t, side],
+                recv_sem=halo_recv.at[t, side],
+                device_id={"dom": device},
+                device_id_type=MESH,
+            )
+            wanted = frame(t) + (side - 1)
+            held = (wanted >= 0) & (wanted < domains)
+            sides.append((copy, inside & (device != dom), held & (wanted != spot)))
+        return sides
 
     def shares(t):
         return [
@@ -269,25 +346,29 @@
             for k in range(domains - 1)
         ]
 
-    has_lower = dom > 0
-    has_upper = dom < domains - 1
-
     def evaluate(t, carry):
         @pl.when(t > 0)
         def _():
-            speeds = v_ref[...] + (0.5 * DT) * mass[...] * f_ref[...]
-            v_ref[...] = speeds
-            x_ref[...] = x_ref[...] + DT * speeds
-        now = x_ref[...]
-        scaled = [KAPPA * now[:, c * BLK:(c + 1) * BLK] for c in range(3)]
+            speeds = v_ref[role] + (0.5 * DT) * mass[role] * f_ref[...]
+            v_ref[role] = speeds
+            x_ref[role] = x_ref[role] + DT * speeds
+        here = x_ref[role]
+        scaled = [KAPPA * here[:, c * BLK:(c + 1) * BLK] for c in range(3)]
         norm = -0.5 * (scaled[0] * scaled[0] + scaled[1] * scaled[1] + scaled[2] * scaled[2])
         for c, rows in enumerate(scaled + [norm]):
-            near[t, pl.ds(rows_slab + c, blocks, stride=4), :] = rows
-        down, up = halo(t)
-        pl.when(has_lower)(down.start)
-        pl.when(has_upper)(up.start)
+            near[t, pl.ds(mine_at(t) + c, blocks, stride=4), :] = rows
+        sides = halo(t)
+        for side in (0, 2, 1):
+            pl.when(sides[side][1])(sides[side][0].start)
+        closing = (t == last) & moved
+
+        @pl.when(closing)
+        def _():
+            for copy in twin_state:
+                copy.start()
+
         for k in range(2):
-            product = weights[k] * now
+            product = weights[role, k] * here
             folded = product[:8] + product[8:]
             folded = folded[:, :BLK] + folded[:, BLK:2 * BLK] + folded[:, 2 * BLK:]
             partial[t, 0, k:k + 1, :] = jnp.sum(folded, axis=0, keepdims=True)
@@ -298,22 +379,42 @@
         def _():
             for copy in moved_v:
                 copy.wait_recv()
+            pl.when(moved)(twin_v.wait_recv)
             choose_all(raw_v, v_ref)
 
-        def block_rows(b):
-            four = near[t, 4 * b:4 * b + 4, :]
-            return jnp.concatenate([four, four], axis=0)
-
+        pl.when(sides[1][2])(sides[1][0].wait_recv)
         for b in range(blocks):
-            rows = block_rows(blocks + b)
+            four = near[t, 4 * (blocks + b):4 * (blocks + b) + 4, :]
+            rows = jnp.concatenate([four, four], axis=0)
             partners_tab[blocks + b] = partner_rows(jnp.where(line == 7, 1.0, rows), line)
             owners_tab[b] = owner_rows(
                 jnp.where(line == 3, 1.0, jnp.where(line == 7, rows + LOG2_EPS, rows)), line
             )
-        pl.when(has_lower)(up.wait_recv)
-        pl.when(has_upper)(down.wait_recv)
-        for b in list(range(blocks)) + list(range(2 * blocks, 3 * blocks)):
-            partners_tab[b] = partner_rows(jnp.where(line == 7, 1.0, block_rows(b)), line)
+
+        def build(first):
+            for b in range(blocks):
+                four = near[t, pl.ds(pl.multiple_of(4 * (first + b), 4), 4), :]
+                rows = jnp.concatenate([four, four], axis=0)
+                partners_tab[first + b] = partner_rows(jnp.where(line == 7, 1.0, rows), line)
+
+        parity = lax.rem(frame(t), 2)
+        odd = parity == 1
+        even = jnp.logical_not(odd)
+        lower, upper = sides[0], sides[2]
+        pl.when(lower[2] & odd)(lower[0].wait_recv)
+        pl.when(upper[2] & even)(upper[0].wait_recv)
+        build(2 * blocks * (1 - parity))
+        pl.when(lower[2] & even)(lower[0].wait_recv)
+        pl.when(upper[2] & odd)(upper[0].wait_recv)
+        build(2 * blocks * parity)
+        held = jnp.where(t == last, 0, role)
+
+        @pl.when(closing)
+        def _():
+            for copy in twin_state:
+                copy.wait_recv()
+
+        now = x_ref[held]
 
         def add_tiles(group, carry):
             for u in range(UNROLL):
@@ -321,8 +422,8 @@
                 sums = two_tiles(
                     partners_tab,
                     owners_tab,
-                    [pair_other[0, first + k] for k in range(2)],
-                    [pair_own[0, first + k] for k in range(2)],
+                    [named[held, 1, first + k] for k in range(2)],
+                    [named[held, 0, first + k] for k in range(2)],
                 )
                 for k in range(2):
                     tiles[pl.ds(pl.multiple_of(16 * (first + k), 16), 16), :] = sums[k]
@@ -338,7 +439,7 @@
         )
         pair = jnp.zeros((blocks, 4 * BLK), jnp.float32)
         for piece in split3(listed_rows):
-            pair = pair + jnp.dot(table[...], piece, preferred_element_type=jnp.float32)
+            pair = pair + jnp.dot(table[held], piece, preferred_element_type=jnp.float32)
         total = pair[:, 3 * BLK:]
         force = now * jnp.concatenate([total, total, total], axis=1) - (1.0 / KAPPA) * pair[:, :3 * BLK]
         for copy in sent:
@@ -348,26 +449,31 @@
             share = share + partial[t, k]
         for k in range(2):
             value = jnp.sum(share[k:k + 1], axis=1, keepdims=True)
-            force = force - (stiffness[0:1, k:k + 1] * (value - centre[k:k + 1, 0:1])) * weights[k]
+            force = force - (stiffness[0:1, k:k + 1] * (value - centre[k:k + 1, 0:1])) * weights[held, k]
         f_ref[...] = force
         @pl.when(t > 0)
         def _():
-            v_ref[...] = v_ref[...] + (0.5 * DT) * mass[...] * force
+            v_ref[held] = v_ref[held] + (0.5 * DT) * mass[held] * force
 
         return carry
 
     lax.fori_loop(0, EVALS, evaluate, 0)
 
-    state_out[0:blocks, :] = x_ref[...]
-    state_out[blocks:2 * blocks, :] = v_ref[...]
+    state_out[0:blocks, :] = x_ref[0]
+    state_out[blocks:2 * blocks, :] = v_ref[0]
     state_out[2 * blocks:3 * blocks, :] = f_ref[...]
 
     for copy in moved_meta + moved_x + moved_v:
         copy.wait_send()
+
+    @pl.when(moved)
+    def _():
+        for copy in [twin_x, twin_v] + twin_rest + twin_state:
+            copy.wait_send()
+
     for t in range(EVALS):
-        down, up = halo(t)
-        pl.when(has_lower)(down.wait_send)
-        pl.when(has_upper)(up.wait_send)
+        for copy, sent_now, _ in halo(t):
+            pl.when(sent_now)(copy.wait_send)
         for copy in shares(t):
             copy.wait_send()
 
@@ -416,40 +522,46 @@
             jax.ShapeDtypeStruct((3 * blocks, wide), f32),
             jax.ShapeDtypeStruct((blocks, BLK), jnp.int32),
         ),
-        in_specs=[anywhere] * 13,
+        in_specs=[anywhere] * 12,
         out_specs=(vmem, vmem),
         scratch_shapes=[
             VMEM((blocks, BLK), f32),
             VMEM((6 * blocks, BLK), f32),
             VMEM((blocks, BLK), jnp.int32),
             VMEM((1, slots), jnp.int32),
+            VMEM((1, slots), jnp.int32),
             VMEM((1, 2), f32),
             VMEM((1, 2), f32),
             VMEM((1, 1), jnp.int32),
             VMEM((1, 1), jnp.int32),
             VMEM((1, 1), jnp.int32),
-            SMEM((1, slots), jnp.int32),
-            SMEM((1, slots), jnp.int32),
+            SMEM((2, 8, BLK), jnp.int32),
+            VMEM((3 * blocks, BLK), f32),
+            VMEM((3 * blocks, BLK), f32),
             VMEM((4, 3 * blocks, BLK), f32),
             VMEM((4, 3 * blocks, BLK), f32),
             VMEM((4, 8, BLK), f32),
-            VMEM((3 * blocks, BLK), f32),
-            VMEM((blocks, wide), f32),
-            VMEM((blocks, wide), f32),
+            VMEM((2, 3 * blocks, BLK), f32),
+            VMEM((2, blocks, wide), f32),
+            VMEM((2, blocks, wide), f32),
             VMEM((blocks, wide), f32),
             VMEM((EVALS, 12 * blocks, BLK), f32),
+            VMEM((2, 2, blocks, wide), f32),
             VMEM((2, blocks, wide), f32),
-            VMEM((blocks, wide), f32),
-            VMEM((blocks, slots), jnp.bfloat16),
+            VMEM((2, 8, BLK), jnp.int32),
+            VMEM((2, blocks, slots), jnp.bfloat16),
             VMEM((16 * slots, BLK), f32),
             VMEM((3 * blocks, 32, BLK), jnp.bfloat16),
             VMEM((blocks, 32, BLK), jnp.bfloat16),
             VMEM((EVALS, domains, 2, BLK), f32),
-            dma((13,)),
+            dma((12,)),
+            dma((2,)),
             dma((3, 3)),
             dma((3, 3)),
-            dma((EVALS, 2)),
-            dma((EVALS, 2)),
+            dma((7,)),
+            dma((7,)),
+            dma((EVALS, 3)),
+            dma((EVALS, 3)),
             dma((EVALS, domains - 1)),
             dma((EVALS, domains - 1)),
         ],
@@ -463,13 +575,12 @@
         cv_weight.reshape(2, 3, blocks, BLK).transpose(1, 2, 0, 3).reshape(6 * blocks, BLK),
         block_order.reshape(blocks, BLK),
         pair_own,
+        pair_other,
         stiffness[None],
         centers[0],
         pair_count[None],
         accept_row,
         accept_col,
-        pair_own,
-        pair_other,
         ))
     )
     outs = pl.pallas_call(

time: 29.1 us -> 27.7 us (0.952)
  Pallas kernels: 26.3 us -> 24.9 us
    pallas_call x1, Pallas kernels: 25.3 us -> 23.9 us  [per_device(): pl.pallas_call(functools.partial(simulate, domains, slots), out_shape=(ja...]
where the time goes in v5:
time: 27.7 us; the launch traced here: 27.5 us
  Pallas kernels  24.9 us (90%)
  between operations  2.58 us (9%)
    pallas_call x1, Pallas kernels, per_device(): pl.pallas_call(functools.partial(simulate, domains, slots), out_shape=(ja...  23.9 us
    pallas_call x1, Pallas kernels, per_device(): pl.pallas_call(restore, out_shape=(jax.ShapeDtypeStruct((3 * blocks, BLK)...  1.04 us

profile of v5, /device:TPU:1, one launch (start us, length us, event | category | flops | bytes accessed | tf_op | source)
XLA Modules:
  0.0 27.5 jit_solution(17923607282472994467)
XLA Ops:
  2.6 23.9 %simulate.1 = (f32[48,384]{1,0:T(8,128)S(1)}, s32[16,128]{1,0:T(8,128)S(1)}) custom-call(f32[48,128]{1,0:T(8,128)} %bitcast.17, f32[48,128]{1,0:T(8,128)} %bitcast.18, f32[16,128]{1,0:T(8,128)} %bitcast.19, f32[96,128]{1,0:T(8,128)} %bitcast.16, s32[16,128]{1,0:T(8,128)} %bitcast.20, s32[1,64]{1,0:T(1,128)} %refs_5_.1, s32[1,64]{1,0:T(1,128)} %refs_6_.1, ...), custom_call_target="tpu_custom_call" | custom-call | tf_op jit(solution)/shard_map/simulate/pallas_call | solution.py:519
  26.5 1.0 %restore.1 = (f32[48,128]{1,0:T(8,128)}, f32[48,128]{1,0:T(8,128)}, f32[48,128]{1,0:T(8,128)}) custom-call(f32[48,384]{1,0:T(8,128)S(1)} %get-tuple-element.8.state, s32[16,128]{1,0:T(8,128)S(1)} %get-tuple-element.9.inverse), custom_call_target="tpu_custom_call" | custom-call | tf_op jit(solution)/shard_map/restore/pallas_call | solution.py:586

commit v6 on v5

--- a/solution.py
+++ b/solution.py
@@ -545,12 +545,12 @@
             VMEM((2, blocks, wide), f32),
             VMEM((2, blocks, wide), f32),
             VMEM((blocks, wide), f32),
-            VMEM((EVALS, 12 * blocks, BLK), f32),
+            VMEM((EVALS, 12 * blocks + 8, BLK), f32),
             VMEM((2, 2, blocks, wide), f32),
             VMEM((2, blocks, wide), f32),
             VMEM((2, 8, BLK), jnp.int32),
             VMEM((2, blocks, slots), jnp.bfloat16),
-            VMEM((16 * slots, BLK), f32),
+            VMEM((16 * slots + 16, BLK), f32),
             VMEM((3 * blocks, 32, BLK), jnp.bfloat16),
             VMEM((blocks, 32, BLK), jnp.bfloat16),
             VMEM((EVALS, domains, 2, BLK), f32),

time: 27.7 us -> 27.7 us (level)
  no operation moved by 1% of the time
where the time goes in v6:
time: 27.7 us; the launch traced here: 27.5 us
  Pallas kernels  24.9 us (90%)
  between operations  2.58 us (9%)
    pallas_call x1, Pallas kernels, per_device(): pl.pallas_call(functools.partial(simulate, domains, slots), out_shape=(ja...  23.9 us
    pallas_call x1, Pallas kernels, per_device(): pl.pallas_call(restore, out_shape=(jax.ShapeDtypeStruct((3 * blocks, BLK)...  1.04 us

profile of v6, /device:TPU:1, one launch (start us, length us, event | category | flops | bytes accessed | tf_op | source)
XLA Modules:
  0.0 27.5 jit_solution(16327899644686717564)
XLA Ops:
  2.6 23.9 %simulate.1 = (f32[48,384]{1,0:T(8,128)S(1)}, s32[16,128]{1,0:T(8,128)S(1)}) custom-call(f32[48,128]{1,0:T(8,128)} %bitcast.17, f32[48,128]{1,0:T(8,128)} %bitcast.18, f32[16,128]{1,0:T(8,128)} %bitcast.19, f32[96,128]{1,0:T(8,128)} %bitcast.16, s32[16,128]{1,0:T(8,128)} %bitcast.20, s32[1,64]{1,0:T(1,128)} %refs_5_.1, s32[1,64]{1,0:T(1,128)} %refs_6_.1, ...), custom_call_target="tpu_custom_call" | custom-call | tf_op jit(solution)/shard_map/simulate/pallas_call | solution.py:519
  26.5 1.0 %restore.1 = (f32[48,128]{1,0:T(8,128)}, f32[48,128]{1,0:T(8,128)}, f32[48,128]{1,0:T(8,128)}) custom-call(f32[48,384]{1,0:T(8,128)S(1)} %get-tuple-element.8.state, s32[16,128]{1,0:T(8,128)S(1)} %get-tuple-element.9.inverse), custom_call_target="tpu_custom_call" | custom-call | tf_op jit(solution)/shard_map/restore/pallas_call | solution.py:586
